TPU v7x, 32 devices: a whole 2x2x4 slice. The times are simulated.
32 devices in a mesh: ens: 4 (over y, x), lat: 2 (over core), lon: 4 (over z).
Axes of the slice: x: 2, y: 2, z: 4, core: 2. Of those that a mesh axis runs over, the one named last changes fastest.
Arguments:
- fields: bfloat16 [8, 36, 96, 384], P('ens', 'lat', 'lon'), parts along dimension 0, may hold values from -6 to 6
- region_ids: int32 [2, 36, 96], P(None, 'lat', 'lon'), may hold values from 0 to 3
- bias_index: int32 [144, 144], replicated, may hold values from 0 to 3311
- earth_bias: bfloat16 [6, 3312, 12], P('lat'), may hold values from -70 to 170
- w_qkv: bfloat16 [384, 1152], replicated, may hold values from -0.3125 to 0.3125
- w_proj: bfloat16 [384, 384], replicated, may hold values from -0.3125 to 0.3125
- w_fc1: bfloat16 [384, 1536], replicated, may hold values from -0.3125 to 0.3125
- w_fc2: bfloat16 [1536, 384], replicated, may hold values from -0.15625 to 0.15625
Outputs:
- result: bfloat16 [8, 36, 96, 384], P('ens', 'lat', 'lon'), parts along dimension 0
There are 4 independent parts, one for each index of `ens`. A program takes and returns all parts, laid end to end along the dimension named above; an argument that names none is the same for every part. Nothing has to cross between parts.
All inputs are finite; a program needn't handle non-finite values.
Results may differ from a plain program's by a relative error of at most 0.009.
Values may be sent and summed in bfloat16 or wider, within the bound.
A program may use at most 128 MiB of HBM per device.

v0:
```python
import functools
import math

import jax
import jax.numpy as jnp
from jax import lax
from jax.experimental import pallas as pl
from jax.experimental.pallas import tpu as pltpu
from jax.sharding import PartitionSpec as P

WZ = 2
WLAT = 6
WLON = 12
EPS_NORM = 1e-05
LOG2E = math.log2(math.e)
LO = 256
LANES = 128
AT_ONCE = 4
GRANT = 32 * 1024 * 1024
NT = (((1,), (1,)), ((), ()))


def norm_rows(wide):
    average = jnp.mean(wide, axis=-1, keepdims=True)
    centred = wide - average
    spread = jnp.mean(centred * centred, axis=-1, keepdims=True)
    return (centred * lax.rsqrt(spread + EPS_NORM)).astype(jnp.bfloat16)


def bias_kernel(slab, with_rest, *refs):
    main_idx, table, out = refs[0], refs[-2], refs[-1]
    tokens = main_idx.shape[0]
    step = out.shape[0] // slab
    pieces = table.shape[0] // slab
    low = lax.broadcasted_iota(jnp.int32, (LO, LANES), 0)

    def lookup(lines):
        spots = [jnp.where(low == (row & (LO - 1)), 1.0, 0.0).astype(jnp.bfloat16) for row in lines]
        found = jnp.dot(
            table[...], jnp.concatenate(spots, axis=1), preferred_element_type=jnp.float32
        )
        picked = []
        for place, row in enumerate(lines):
            high = row // LO
            columns = found[:, place * LANES : (place + 1) * LANES]
            total = columns[(pieces - 1) * slab :]
            for piece in range(pieces - 1):
                total = jnp.where(high == piece, columns[piece * slab : (piece + 1) * slab], total)
            picked.append(total * LOG2E)
        return picked

    @pl.loop(0, tokens // 8)
    def _(block):
        rows = main_idx[pl.ds(pl.multiple_of(block * 8, 8), 8), :]
        for start in range(0, 8, AT_ONCE):
            lines = [rows[start + line : start + line + 1] for line in range(AT_ONCE)]
            for line, values in enumerate(lookup(lines)):
                out[pl.ds(block * 8 + start + line, slab, stride=step), :] = values

    if not with_rest:
        return
    rest_idx = refs[1]
    rest = rest_idx.shape[0]

    @pl.loop(0, rest // 8)
    def _(block):
        rows = rest_idx[pl.ds(pl.multiple_of(block * 8, 8), 8), :]
        for start in range(0, 8, AT_ONCE // 2):
            lines = []
            for line in range(start, start + AT_ONCE // 2):
                lines += [rows[line : line + 1, :LANES], rows[line : line + 1, LANES:]]
            for line, values in enumerate(lookup(lines)):
                base = tokens + rest * (line % 2)
                out[pl.ds(base + block * 8 + start + line // 2, slab, stride=step), :] = values


def bias_tables(earth_bias, bias_index):
    bands, positions, heads = earth_bias.shape
    tokens = bias_index.shape[0]
    rest = tokens - LANES
    count = bands * heads
    slab = -(-count // 8) * 8
    pieces = -(-positions // LO)
    table = earth_bias.transpose(0, 2, 1).reshape(count, positions)
    table = jnp.pad(table, ((0, slab - count), (0, pieces * LO - positions)))
    table = table.reshape(slab, pieces, LO).transpose(1, 0, 2).reshape(pieces * slab, LO)
    main_idx = bias_index[:LANES].T
    rest_idx = jnp.pad(bias_index[LANES:], ((0, 0), (0, 2 * LANES - tokens)))
    half = tokens // 2

    def call(with_rest, rows, *args):
        return pl.pallas_call(
            functools.partial(bias_kernel, slab, with_rest),
            out_shape=jax.ShapeDtypeStruct((slab * rows, LANES), jnp.float32),
            compiler_params=pltpu.CompilerParams(vmem_limit_bytes=GRANT // 2),
            cost_estimate=pl.CostEstimate(
                flops=table.size * tokens * tokens, bytes_accessed=slab * tokens * tokens * 2,
                transcendentals=0,
            ),
            name="bias_lookup",
        )(*args, table)

    first = call(False, half, main_idx[:half])
    return first, lambda: call(True, half + 2 * rest, main_idx[half:], rest_idx)


def attend_window(heads, normed, query, key, row, bias_first, bias_second, w_vt, turned):
    tokens, width = normed.shape
    dim = width // heads
    per = LANES // dim
    rest = tokens - LANES
    scale = dim ** (-0.5) * LOG2E
    value_t = lax.dot_general(w_vt[...], normed, NT, preferred_element_type=jnp.float32)
    value_t = value_t.astype(jnp.bfloat16)
    row = row.astype(jnp.float32)
    diagonal = lax.broadcasted_iota(jnp.int32, (tokens, tokens), 0) == lax.broadcasted_iota(
        jnp.int32, (tokens, tokens), 1
    )
    col = jnp.sum(jnp.where(diagonal, row, 0.0), axis=1, keepdims=True)
    half = tokens // 2
    step = half + 2 * rest
    barred = jnp.where(col == row[:, :LANES], 0.0, -jnp.inf)
    owner = lax.broadcasted_iota(jnp.int32, (LANES, LANES), 1) // dim
    zero = jnp.zeros((), jnp.bfloat16)
    for group in range(width // LANES):
        span = slice(group * LANES, (group + 1) * LANES)
        asked = query[:LANES, span]
        stacked = jnp.concatenate([jnp.where(owner == h, asked, zero) for h in range(per)], axis=0)
        raw = lax.dot_general(key[:, span], stacked, NT, preferred_element_type=jnp.float32)
        for h in range(per):
            head = group * per + h
            scores = raw[:, h * LANES : (h + 1) * LANES] * scale
            bias = [bias_first[head * half : (head + 1) * half, :]]
            bias += [bias_second[head * step : head * step + half, :]]
            bias = jnp.concatenate(bias, axis=0)
            scores = scores + bias + barred
            grown = jnp.exp2(scores - jnp.max(scores, axis=0, keepdims=True))
            total = jnp.sum(grown, axis=0, keepdims=True)
            mixed = jnp.dot(
                value_t[head * dim : (head + 1) * dim],
                grown.astype(jnp.bfloat16),
                preferred_element_type=jnp.float32,
            )
            turned[head * dim : (head + 1) * dim, :] = mixed / total
    owner = lax.broadcasted_iota(jnp.int32, (rest, width), 1) // dim
    asked = query[LANES:]
    stacked = jnp.concatenate([jnp.where(owner == h, asked, zero) for h in range(heads)], axis=0)
    scores = lax.dot_general(stacked, key, NT, preferred_element_type=jnp.float32) * scale
    left = [bias_second[h * step + half : h * step + half + rest, :] for h in range(heads)]
    right = [bias_second[h * step + half + rest : (h + 1) * step, :] for h in range(heads)]
    left, right = jnp.concatenate(left, axis=0), jnp.concatenate(right, axis=0)
    scores = scores + jnp.concatenate([left, right[:, : tokens - LANES]], axis=1)
    barred = jnp.where(col[LANES:] == row, 0.0, -jnp.inf)
    scores = scores + jnp.concatenate([barred] * heads, axis=0)
    grown = jnp.exp2(scores - jnp.max(scores, axis=1, keepdims=True))
    total = jnp.sum(grown, axis=1, keepdims=True)
    mixed = lax.dot_general(
        grown.astype(jnp.bfloat16), value_t, NT, preferred_element_type=jnp.float32
    )
    mixed = mixed / total
    last = jnp.zeros((rest, width), jnp.float32)
    for h in range(heads):
        last = jnp.where(owner == h, mixed[h * rest : (h + 1) * rest], last)
    return jnp.concatenate([turned[...].T, last], axis=0).astype(jnp.bfloat16)


def layer_kernel(heads, together, x, *refs):
    blocks, refs = refs[: 3 * together], refs[3 * together :]
    away, out, turned, here, sems = refs[:5], refs[5], refs[6], refs[7:12], refs[12]
    w_qkv, w_vt, w_proj, w_fc1, w_fc2 = here
    away = (away[0].at[:, : w_qkv.shape[1]], *away[1:])
    copies = [
        pltpu.make_async_copy(source, target, sems.at[i])
        for i, (source, target) in enumerate(zip(away, here))
    ]
    opening = pl.program_id(0) == 0

    @pl.when(opening)
    def _():
        for copy in copies:
            copy.start()

    tokens, width = x.shape[1:]
    fields = x[...].reshape(together * tokens, width)
    normed = norm_rows(fields)

    @pl.when(opening)
    def _():
        copies[0].wait()
        copies[1].wait()

    packed = jnp.dot(normed, w_qkv[...], preferred_element_type=jnp.float32)
    packed = packed.astype(jnp.bfloat16)
    contexts = []
    for place in range(together):
        rows = slice(place * tokens, (place + 1) * tokens)
        contexts.append(
            attend_window(
                heads, normed[rows], packed[rows, :width], packed[rows, width:],
                blocks[3 * place][0], *blocks[3 * place + 1 : 3 * place + 3], w_vt, turned.at[place],
            )
        )

    @pl.when(opening)
    def _():
        for copy in copies[2:]:
            copy.wait()

    context = jnp.concatenate(contexts, axis=0)
    projected = jnp.dot(context, w_proj[...], preferred_element_type=jnp.float32)
    projected = projected.astype(jnp.bfloat16).astype(jnp.float32)
    residual = (fields + projected).astype(jnp.bfloat16).astype(jnp.float32)
    normed = norm_rows(residual)
    grown = jnp.dot(normed, w_fc1[...], preferred_element_type=jnp.float32)
    hidden = (0.5 * grown * (1.0 + lax.erf(grown * math.sqrt(0.5)))).astype(jnp.bfloat16)
    summed = residual + jnp.dot(hidden, w_fc2[...], preferred_element_type=jnp.float32)
    out[...] = summed.reshape(out.shape)


def layer(windows, regions, tables, where_of, per_band, heads, w_qkv, w_vt, w_proj, w_fc1, w_fc2):
    count, tokens, width = windows.shape
    together = 2 if count % 2 == 0 else 1
    slab = -(-heads * (regions.shape[0] // per_band) // 8) * 8
    specs, args = [], []
    for place in range(together):
        window = lambda w, place=place: (where_of(w * together + place), 0, 0)
        band = lambda w, place=place: (where_of(w * together + place) // per_band, 0)
        specs.append(pl.BlockSpec((1, 1, tokens), window))
        args.append(regions)
        for table in tables:
            rows = table.shape[0] // slab
            specs.append(pl.BlockSpec((heads * rows, LANES), band))
            args.append(table)
    weights = (w_qkv, w_vt, w_proj, w_fc1, w_fc2)
    return pl.pallas_call(
        functools.partial(layer_kernel, heads, together),
        grid=(count // together,),
        out_shape=jax.ShapeDtypeStruct(windows.shape, jnp.float32),
        in_specs=[
            pl.BlockSpec((together, tokens, width), lambda w: (w, 0, 0)),
            *specs,
            *[pl.BlockSpec(memory_space=pltpu.HBM)] * len(weights),
        ],
        out_specs=pl.BlockSpec((together, tokens, width), lambda w: (w, 0, 0)),
        scratch_shapes=[
            pltpu.VMEM((together, width, LANES), jnp.float32),
            pltpu.VMEM((width, 2 * width), w_qkv.dtype),
            *[pltpu.VMEM(weight.shape, weight.dtype) for weight in weights[1:]],
            pltpu.SemaphoreType.DMA((len(weights),)),
        ],
        compiler_params=pltpu.CompilerParams(vmem_limit_bytes=GRANT),
        cost_estimate=pl.CostEstimate(
            flops=2 * count * tokens * (w_qkv.size + w_proj.size + w_fc1.size + w_fc2.size) * 3,
            bytes_accessed=windows.size * 4 + w_fc1.size * 8,
            transcendentals=count * heads * tokens * tokens,
        ),
        name="layer",
    )(windows, *args, *weights)


def from_behind(value, axis, steps):
    count = lax.axis_size(axis)
    pairs = [(source, (source + steps) % count) for source in range(count)]
    return lax.ppermute(value, axis, pairs)


def from_corner(value, steps):
    lats, lons = lax.axis_size("lat"), lax.axis_size("lon")
    pairs = [
        (a * lons + o, (a + steps) % lats * lons + (o + steps) % lons)
        for a in range(lats)
        for o in range(lons)
    ]
    return lax.ppermute(value, ("lat", "lon"), pairs)


def pack_kernel(fields, cols, rows, corner):
    half_lat = rows.shape[1]
    lons = cols.shape[2]
    cols[...] = fields[:, half_lat:, :lons, :]
    rows[...] = fields[:, :half_lat]
    corner[...] = fields[:, :half_lat, :lons, :]


def window_slot(lat_wins, lon_wins, t, b):
    if t == lat_wins - 1:
        return 0, lat_wins - 1 + b
    if b == lon_wins - 1:
        return 0, t
    return 1, t * (lon_wins - 1) + b


def spread_kernel(fields, cols, rows, corner, *outs):
    levels, lat_rows, lon_cols, width = fields.shape
    half_lat, half_lon = WLAT // 2, WLON // 2
    lat_wins, lon_wins = lat_rows // WLAT, lon_cols // WLON
    for level in range(levels):
        source = (level + WZ // 2) % levels
        for a in range(lat_rows):
            away = a - (lat_rows - half_lat)
            own = fields[source, a + half_lat] if away < 0 else rows[source, away]
            halo = cols[source, a] if away < 0 else corner[source, away]
            line = [own.astype(jnp.float32)[half_lon:], halo.astype(jnp.float32)[:half_lon]]
            line = jnp.concatenate(line, axis=0)
            place = (level * WLAT + a % WLAT) * WLON
            for b in range(lon_wins):
                which, slot = window_slot(lat_wins, lon_wins, a // WLAT, b)
                outs[which][slot, place : place + WLON, :] = line[b * WLON : (b + 1) * WLON]


def window_row(wins, lat_wins, lon_wins, level, a):
    place = (level * WLAT + a % WLAT) * WLON
    parts = []
    for b in range(lon_wins):
        which, slot = window_slot(lat_wins, lon_wins, a // WLAT, b)
        parts.append(wins[which][slot, place : place + WLON, :])
    return parts


def back_kernel(lat_wins, lon_wins, edge, cols, rows, corner):
    levels, upper, spare = cols.shape[:3]
    half_lon = WLON // 2
    for level in range(levels):
        target = (level + WZ // 2) % levels
        for a in range(lat_wins * WLAT):
            which, slot = window_slot(lat_wins, lon_wins, a // WLAT, lon_wins - 1)
            place = (level * WLAT + a % WLAT) * WLON
            last = edge[slot, place : place + WLON, :]
            sent = jnp.concatenate([last[half_lon:], last[: spare - half_lon]], axis=0)
            if a < upper:
                cols[target, a] = sent.astype(jnp.bfloat16)
            else:
                corner[target, a - upper] = sent.astype(jnp.bfloat16)
                line = window_row((edge,), lat_wins, lon_wins, level, a)
                rows[target, a - upper] = jnp.concatenate(line, axis=0).astype(jnp.bfloat16)


def join_kernel(*refs):
    wins, (cols, rows, corner, out) = refs[:-4], refs[-4:]
    levels, lat_rows, lon_cols, width = out.shape
    half_lat, half_lon = WLAT // 2, WLON // 2
    lat_wins, lon_wins = lat_rows // WLAT, lon_cols // WLON
    for level in range(levels):
        target = (level + WZ // 2) % levels
        for a in range(-half_lat, lat_rows - half_lat):
            if a < 0:
                halo = corner[target, a + half_lat].astype(jnp.float32)
                kept = rows[target, a + half_lat].astype(jnp.float32)
            else:
                halo = cols[target, a].astype(jnp.float32)
                kept = jnp.concatenate(window_row(wins, lat_wins, lon_wins, level, a), axis=0)
            line = jnp.concatenate([halo[:half_lon], kept[: lon_cols - half_lon]], axis=0)
            out[target, a + half_lat] = line.astype(jnp.bfloat16)


def small(kernel, shapes, name, *args):
    size = sum(arg.size for arg in args)
    return pl.pallas_call(
        kernel,
        out_shape=shapes,
        compiler_params=pltpu.CompilerParams(vmem_limit_bytes=GRANT // 2),
        cost_estimate=pl.CostEstimate(flops=size, bytes_accessed=4 * size, transcendentals=0),
        name=name,
    )(*args)


def local(fields, region_ids, bias_index, earth_bias, w_qkv, w_proj, w_fc1, w_fc2):
    levels, lat_rows, lon_cols, width = fields.shape
    lat_wins = lat_rows // WLAT
    lon_wins = lon_cols // WLON
    tokens = levels * WLAT * WLON
    half_lat = WLAT // 2
    heads = earth_bias.shape[-1]
    spare = -(-(WLON // 2) // 8) * 8
    halo_shapes = tuple(
        jax.ShapeDtypeStruct((levels, lats, lons, width), jnp.bfloat16)
        for lats, lons in ((lat_rows - half_lat, spare), (half_lat, lon_cols), (half_lat, spare))
    )
    first, second_call = bias_tables(earth_bias, bias_index)
    halos = small(pack_kernel, halo_shapes, "pack", fields)
    first, *halos = lax.optimization_barrier((first, *halos))
    cols = from_behind(halos[0], "lon", -1)
    rows = from_behind(halos[1], "lat", -1)
    corner = from_corner(halos[2], -1)
    tables = (first, second_call())
    regions = region_ids.reshape(levels, lat_wins, WLAT, lon_wins, WLON)
    regions = regions.transpose(1, 3, 0, 2, 4).reshape(lat_wins * lon_wins, 1, tokens)
    counts = [lat_wins - 1 + lon_wins, (lat_wins - 1) * (lon_wins - 1)]
    window_shapes = tuple(
        jax.ShapeDtypeStruct((count, tokens, width), jnp.float32) for count in counts if count
    )
    windows = small(spread_kernel, window_shapes, "spread", fields, cols, rows, corner)
    weights = (w_qkv, w_qkv[:, 2 * width :].T, w_proj, w_fc1, w_fc2)
    last = lat_wins - 1
    results = [
        layer(
            windows[0], regions, tables,
            lambda w: jnp.where(w < last, (w + 1) * lon_wins - 1, last * lon_wins + w - last),
            lon_wins, heads, *weights,
        )
    ]
    halos = small(
        functools.partial(back_kernel, lat_wins, lon_wins), halo_shapes, "pack_back", results[0]
    )
    cols = from_behind(halos[0], "lon", 1)
    rows = from_behind(halos[1], "lat", 1)
    corner = from_corner(halos[2], 1)
    if len(windows) > 1:
        inner = lon_wins - 1
        results.append(
            layer(
                windows[1], regions, tables,
                lambda w: w // inner * lon_wins + w % inner, lon_wins, heads, *weights,
            )
        )
    shape = jax.ShapeDtypeStruct(fields.shape, jnp.bfloat16)
    return small(join_kernel, shape, "join", *results, cols, rows, corner)


def solution(mesh):
    return jax.shard_map(
        local,
        mesh=mesh,
        in_specs=(
            P("ens", "lat", "lon", None),
            P(None, "lat", "lon"),
            P(),
            P("lat", None, None),
            P(),
            P(),
            P(),
            P(),
        ),
        out_specs=P("ens", "lat", "lon", None),
        check_vma=False,
    )
```

profile of v0, /device:TPU:0, one launch (start us, length us, event | category | flops | bytes accessed | tf_op | source)
XLA Modules:
  0.0 50.7 jit_solution(1445408319017284099)
XLA Ops:
  0.0 1.0 %slice.15 = s32[128,144]{1,0:T(8,128)S(1)} slice(s32[144,144]{1,0:T(8,128)} %param.10), slice={[0:128], [0:144]} | slice | bytes 147456 | tf_op jit(solution)/shard_map/slice | solution.py:87
  1.0 0.1 copy.20
  1.1 1.1 %reshape.15 = bf16[36,3312]{1,0:T(8,128)(2,1)S(1)} reshape(bf16[3,12,3312]{2,1,0:T(8,128)(2,1)} %bitcast.15) | data formatting | bytes 476928 | tf_op jit(solution)/shard_map/reshape | solution.py:84
  2.2 0.2 reshape.16
  2.4 0.1 copy.13
  2.5 0.7 %pack.1 = (bf16[2,15,8,384]{3,2,1,0:T(8,128)(2,1)}, bf16[2,3,24,384]{3,2,1,0:T(8,128)(2,1)}, bf16[2,3,8,384]{3,2,1,0:T(8,128)(2,1)}) custom-call(bf16[2,18,24,384]{3,2,1,0:T(8,128)(2,1)S(1)} %copy-done.2), custom_call_target="tpu_custom_call" | custom-call | flops 331776 | bytes 1327104 | tf_op jit(solution)/shard_map/pack/pallas_call | solution.py:358
  3.2 5.0 %bias_lookup.2.refs_1_.refs_4_ = f32[2880,128]{1,0:T(8,128)S(1)} custom-call(s32[72,128]{1,0:T(8,128)S(1)} %get-tuple-element.30.refs_0_, bf16[520,256]{1,0:T(8,128)(2,1)S(1)} %bitcast.12), custom_call_target="tpu_custom_call" | custom-call | flops 2760376320 | bytes 1658880 | tf_op jit(solution)/shard_map/bias_lookup/pallas_call | solution.py:92
  8.2 1.1 %copy-done = f32[2880,128]{1,0:T(8,128)} copy-done((f32[2880,128]{1,0:T(8,128)}, f32[2880,128]{1,0:T(8,128)S(1)}, u32[]{:S(2)}) %copy-start) | copy-done | bytes 1474584
  9.4 4.5 %collective-permute-start.2 = (bf16[2,3,8,384]{3,2,1,0:T(8,128)(2,1)}, bf16[2,3,8,384]{3,2,1,0:T(8,128)(2,1)S(1)}, u32[]{:S(2)}, u32[]{:S(2)}) collective-permute-start(bf16[2,3,8,384]{3,2,1,0:T(8,128)(2,1)} %get-tuple-element.22), channel_id=1, source_target_pairs={{0,7},{1,4},{2,5},{3,6},{4,3},{5,0},{6,1},{7,2},{8,15},{9,12},{10,... | collective-permute-start | bytes 110600 | tf_op jit(solution)/shard_map/ppermute | solution.py:274
  13.9 0.7 %collective-permute-start.1 = (bf16[2,3,24,384]{3,2,1,0:T(8,128)(2,1)}, bf16[2,3,24,384]{3,2,1,0:T(8,128)(2,1)S(1)}, u32[]{:S(2)}, u32[]{:S(2)}) collective-permute-start(bf16[2,3,24,384]{3,2,1,0:T(8,128)(2,1)} %get-tuple-element.21), channel_id=1, source_target_pairs={{0,4},{4,0},{1,5},{5,1},{2,6},{6,2},{3,7},{7,3},{8,12},{12,8},{9,1... | collective-permute-start | bytes 331784 | tf_op jit(solution)/shard_map/ppermute | solution.py:264
  14.6 0.4 collective-permute-start
  15.0 0.0 slice-start
  15.0 6.9 %bias_lookup.3.refs_2_.refs_5_ = f32[4160,128]{1,0:T(8,128)S(1)} custom-call(s32[72,128]{1,0:T(8,128)S(1)} %get-tuple-element.29.refs_0_, s32[16,256]{1,0:T(8,128)S(1)} %pad.9.refs_1_, bf16[520,256]{1,0:T(8,128)(2,1)S(1)} %bitcast.13), custom_call_target="tpu_custom_call" | custom-call | flops 2760376320 | bytes 1658880 | tf_op jit(solution)/shard_map/bias_lookup/pallas_call | solution.py:92
  21.9 0.1 reshape.18
  22.0 0.1 reshape.20.refs_0_.refs_3_
  22.1 0.2 copy.21
  22.4 0.0 collective-permute-done.2.corner
  22.4 1.1 %spread.1 = (f32[4,144,384]{2,1,0:T(8,128)S(1)}, f32[2,144,384]{2,1,0:T(8,128)S(1)}) custom-call(bf16[2,18,24,384]{3,2,1,0:T(8,128)(2,1)S(1)} %copy-done.2, bf16[2,15,8,384]{3,2,1,0:T(8,128)(2,1)} %collective-permute-done.cols, bf16[2,3,24,384]{3,2,1,0:T(8,128)(2,1)S(1)} %collective-permute-done.1.rows, bf16[2,3,8,384]{3,2,1,0:T(8,128)(2,1)S(1)} %collective-permute-done.2.corner), custom_call_target="tpu_custom_call" | custom-call | flops 497664 | bytes 1990656 | tf_op jit(solution)/shard_map/spread/pallas_call | solution.py:358
  23.5 1.4 %copy-done.1 = f32[2880,128]{1,0:T(8,128)S(1)} copy-done((f32[2880,128]{1,0:T(8,128)S(1)}, f32[2880,128]{1,0:T(8,128)}, u32[]{:S(2)}) %copy-start.1) | copy-done | bytes 1474584
  24.9 1.2 %copy-done.3 = bf16[384,1152]{1,0:T(8,128)(2,1)S(1)} copy-done((bf16[384,1152]{1,0:T(8,128)(2,1)S(1)}, bf16[384,1152]{1,0:T(8,128)(2,1)}, u32[]{:S(2)}) %copy-start.3) | copy-done | bytes 884760
  26.1 1.3 %copy-done.5 = bf16[384,1536]{1,0:T(8,128)(2,1)S(1)} copy-done((bf16[384,1536]{1,0:T(8,128)(2,1)S(1)}, bf16[384,1536]{1,0:T(8,128)(2,1)}, u32[]{:S(2)}) %copy-start.5) | copy-done | bytes 1179672
  27.3 1.3 %copy-done.7 = bf16[1536,384]{1,0:T(8,128)(2,1)S(1)} copy-done((bf16[1536,384]{1,0:T(8,128)(2,1)S(1)}, bf16[1536,384]{1,0:T(8,128)(2,1)}, u32[]{:S(2)}) %copy-start.7) | copy-done | bytes 1179672
  28.6 1.0 %copy-done.8 = bf16[384,384]{1,0:T(8,128)(2,1)S(1)} copy-done((bf16[384,384]{1,0:T(8,128)(2,1)S(1)}, bf16[384,384]{1,0:T(8,128)(2,1)}, u32[]{:S(2)}) %copy-start.8) | copy-done | bytes 294936
  29.6 9.9 %layer.2.edge.refs_0_ = f32[4,144,384]{2,1,0:T(8,128)S(1)} custom-call(f32[4,144,384]{2,1,0:T(8,128)S(1)} %get-tuple-element.23.x, s32[6,1,144]{2,1,0:T(1,128)S(1)} %reshape.20.refs_0_.refs_3_, f32[2880,128]{1,0:T(8,128)S(1)} %copy-done.1, f32[4160,128]{1,0:T(8,128)S(1)} %bias_lookup.3.refs_2_.refs_5_, s32[6,1,144]{2,1,0:T(1,128)S(1)} %reshape.20.refs_0_.refs_3_, ...), custom_call_target="tpu_custom_call" | custom-call | flops 6115295232 | bytes 5603328 | tf_op jit(solution)/shard_map/layer/pallas_call | solution.py:235
  39.5 0.0 copy-start.4
  39.5 0.1 pack_back.1
  39.6 1.0 %collective-permute-start.5 = (bf16[2,3,8,384]{3,2,1,0:T(8,128)(2,1)S(1)}, bf16[2,3,8,384]{3,2,1,0:T(8,128)(2,1)S(1)}, u32[]{:S(2)}, u32[]{:S(2)}) collective-permute-start(bf16[2,3,8,384]{3,2,1,0:T(8,128)(2,1)S(1)} %get-tuple-element.28), channel_id=1, source_target_pairs={{0,5},{1,6},{2,7},{3,4},{4,1},{5,2},{6,3},{7,0},{8,13},{9,14},{10,... | collective-permute-start | bytes 110600 | tf_op jit(solution)/shard_map/ppermute | solution.py:274
  40.5 0.8 %collective-permute-start.4 = (bf16[2,3,24,384]{3,2,1,0:T(8,128)(2,1)S(1)}, bf16[2,3,24,384]{3,2,1,0:T(8,128)(2,1)S(1)}, u32[]{:S(2)}, u32[]{:S(2)}) collective-permute-start(bf16[2,3,24,384]{3,2,1,0:T(8,128)(2,1)S(1)} %get-tuple-element.27), channel_id=1, source_target_pairs={{0,4},{4,0},{1,5},{5,1},{2,6},{6,2},{3,7},{7,3},{8,12},{12,8},{9,1... | collective-permute-start | bytes 331784 | tf_op jit(solution)/shard_map/ppermute | solution.py:264
  41.3 0.0 collective-permute-start.3
  41.3 5.2 %layer.3.refs_1_ = f32[2,144,384]{2,1,0:T(8,128)S(1)} custom-call(f32[2,144,384]{2,1,0:T(8,128)S(1)} %get-tuple-element.25.x, s32[6,1,144]{2,1,0:T(1,128)S(1)} %reshape.20.refs_0_.refs_3_, f32[2880,128]{1,0:T(8,128)S(1)} %copy-done.1, f32[4160,128]{1,0:T(8,128)S(1)} %bias_lookup.3.refs_2_.refs_5_, s32[6,1,144]{2,1,0:T(1,128)S(1)} %reshape.20.refs_0_.refs_3_, ...), custom_call_target="tpu_custom_call" | custom-call | flops 3057647616 | bytes 5160960 | tf_op jit(solution)/shard_map/layer/pallas_call | solution.py:235
  46.6 3.1 %collective-permute-done.3.refs_2_ = bf16[2,15,8,384]{3,2,1,0:T(8,128)(2,1)S(1)} collective-permute-done((bf16[2,15,8,384]{3,2,1,0:T(8,128)(2,1)S(1)}, bf16[2,15,8,384]{3,2,1,0:T(8,128)(2,1)S(1)}, u32[]{:S(2)}, u32[]{:S(2)}) %collective-permute-start.3) | collective-permute-done | bytes 184352 | tf_op jit(solution)/shard_map/ppermute | solution.py:264
  49.7 1.0 %join.1 = bf16[2,18,24,384]{3,2,1,0:T(8,128)(2,1)} custom-call(f32[4,144,384]{2,1,0:T(8,128)S(1)} %layer.2.edge.refs_0_, f32[2,144,384]{2,1,0:T(8,128)S(1)} %layer.3.refs_1_, bf16[2,15,8,384]{3,2,1,0:T(8,128)(2,1)S(1)} %collective-permute-done.3.refs_2_, bf16[2,3,24,384]{3,2,1,0:T(8,128)(2,1)S(1)} %collective-permute-done.4.refs_3_, ...), custom_call_target="tpu_custom_call" | custom-call | flops 497664 | bytes 1990656 | tf_op jit(solution)/shard_map/join/pallas_call | solution.py:358
  (24 shorter events, 0.1 us)
Async XLA Ops:
  0.0 2.5 %copy-start.2 = (bf16[2,18,24,384]{3,2,1,0:T(8,128)(2,1)S(1)}, bf16[2,18,24,384]{3,2,1,0:T(8,128)(2,1)}, u32[]{:S(2)}) copy-start(bf16[2,18,24,384]{3,2,1,0:T(8,128)(2,1)} %fields.3) | copy-start | bytes 1990660
  3.2 11.8 %slice-start.1 = ((s32[144,144]{1,0:T(8,128)}), s32[16,144]{1,0:T(8,128)S(1)}, s32[]{:S(2)}) async-start(s32[144,144]{1,0:T(8,128)} %param.10), calls=%async_computation.1 | async-start | bytes 32768 | tf_op jit(solution)/shard_map/slice | solution.py:88
  8.2 1.1 %copy-start = (f32[2880,128]{1,0:T(8,128)}, f32[2880,128]{1,0:T(8,128)S(1)}, u32[]{:S(2)}) copy-start(f32[2880,128]{1,0:T(8,128)S(1)} %bias_lookup.2.refs_1_.refs_4_) | copy-start | bytes 4423684
  9.4 13.0 %collective-permute-start.2 = (bf16[2,3,8,384]{3,2,1,0:T(8,128)(2,1)}, bf16[2,3,8,384]{3,2,1,0:T(8,128)(2,1)S(1)}, u32[]{:S(2)}, u32[]{:S(2)}) collective-permute-start(bf16[2,3,8,384]{3,2,1,0:T(8,128)(2,1)} %get-tuple-element.22), channel_id=1, source_target_pairs={{0,7},{1,4},{2,5},{3,6},{4,3},{5,0},{6,1},{7,2},{8,15},{9,12},{10,... | collective-permute-start | bytes 110600 | tf_op jit(solution)/shard_map/ppermute | solution.py:274
  13.9 8.5 %collective-permute-start.1 = (bf16[2,3,24,384]{3,2,1,0:T(8,128)(2,1)}, bf16[2,3,24,384]{3,2,1,0:T(8,128)(2,1)S(1)}, u32[]{:S(2)}, u32[]{:S(2)}) collective-permute-start(bf16[2,3,24,384]{3,2,1,0:T(8,128)(2,1)} %get-tuple-element.21), channel_id=1, source_target_pairs={{0,4},{4,0},{1,5},{5,1},{2,6},{6,2},{3,7},{7,3},{8,12},{12,8},{9,1... | collective-permute-start | bytes 331784 | tf_op jit(solution)/shard_map/ppermute | solution.py:264
  14.6 7.8 %collective-permute-start = (bf16[2,15,8,384]{3,2,1,0:T(8,128)(2,1)}, bf16[2,15,8,384]{3,2,1,0:T(8,128)(2,1)}, u32[]{:S(2)}, u32[]{:S(2)}) collective-permute-start(bf16[2,15,8,384]{3,2,1,0:T(8,128)(2,1)} %get-tuple-element.20), channel_id=1, source_target_pairs={{0,3},{1,0},{2,1},{3,2},{4,7},{5,4},{6,5},{7,6},{8,11},{9,8},{10,9... | collective-permute-start | bytes 552968 | tf_op jit(solution)/shard_map/ppermute | solution.py:264
  15.0 6.9 %copy-start.9 = (s32[2,18,24]{2,0,1:T(2,128)S(1)}, s32[2,18,24]{2,0,1:T(2,128)}, u32[]{:S(2)}) copy-start(s32[2,18,24]{2,0,1:T(2,128)} %param.9) | copy-start | bytes 10372
  15.0 7.1 %slice-start = ((bf16[384,1152]{1,0:T(8,128)(2,1)}), bf16[384,384]{1,0:T(8,128)(2,1)S(1)}, s32[]{:S(2)}) async-start(bf16[384,1152]{1,0:T(8,128)(2,1)} %refs_6_.3), calls=%async_computation | async-start | bytes 589824 | tf_op jit(solution)/shard_map/slice | solution.py:393
  23.5 1.4 %copy-start.1 = (f32[2880,128]{1,0:T(8,128)S(1)}, f32[2880,128]{1,0:T(8,128)}, u32[]{:S(2)}) copy-start(f32[2880,128]{1,0:T(8,128)} %copy-done) | copy-start | bytes 4423684
  24.9 1.2 %copy-start.3 = (bf16[384,1152]{1,0:T(8,128)(2,1)S(1)}, bf16[384,1152]{1,0:T(8,128)(2,1)}, u32[]{:S(2)}) copy-start(bf16[384,1152]{1,0:T(8,128)(2,1)} %refs_6_.3) | copy-start | bytes 2654212
  26.1 1.3 %copy-start.5 = (bf16[384,1536]{1,0:T(8,128)(2,1)S(1)}, bf16[384,1536]{1,0:T(8,128)(2,1)}, u32[]{:S(2)}) copy-start(bf16[384,1536]{1,0:T(8,128)(2,1)} %refs_9_.3) | copy-start | bytes 3538948
  27.3 1.3 %copy-start.7 = (bf16[1536,384]{1,0:T(8,128)(2,1)S(1)}, bf16[1536,384]{1,0:T(8,128)(2,1)}, u32[]{:S(2)}) copy-start(bf16[1536,384]{1,0:T(8,128)(2,1)} %refs_10_.3) | copy-start | bytes 3538948
  28.6 1.0 %copy-start.8 = (bf16[384,384]{1,0:T(8,128)(2,1)S(1)}, bf16[384,384]{1,0:T(8,128)(2,1)}, u32[]{:S(2)}) copy-start(bf16[384,384]{1,0:T(8,128)(2,1)} %refs_8_.3) | copy-start | bytes 884740
  29.6 11.8 %copy-start.6 = (bf16[384,1536]{1,0:T(8,128)(2,1)S(1)}, bf16[384,1536]{1,0:T(8,128)(2,1)}, u32[]{:S(2)}) copy-start(bf16[384,1536]{1,0:T(8,128)(2,1)} %refs_9_.3) | copy-start | bytes 3538948
  39.5 1.9 %copy-start.4 = (bf16[384,1152]{1,0:T(8,128)(2,1)S(1)}, bf16[384,1152]{1,0:T(8,128)(2,1)}, u32[]{:S(2)}) copy-start(bf16[384,1152]{1,0:T(8,128)(2,1)} %refs_6_.3) | copy-start | bytes 2654212
  39.6 7.0 %collective-permute-start.5 = (bf16[2,3,8,384]{3,2,1,0:T(8,128)(2,1)S(1)}, bf16[2,3,8,384]{3,2,1,0:T(8,128)(2,1)S(1)}, u32[]{:S(2)}, u32[]{:S(2)}) collective-permute-start(bf16[2,3,8,384]{3,2,1,0:T(8,128)(2,1)S(1)} %get-tuple-element.28), channel_id=1, source_target_pairs={{0,5},{1,6},{2,7},{3,4},{4,1},{5,2},{6,3},{7,0},{8,13},{9,14},{10,... | collective-permute-start | bytes 110600 | tf_op jit(solution)/shard_map/ppermute | solution.py:274
  40.5 6.1 %collective-permute-start.4 = (bf16[2,3,24,384]{3,2,1,0:T(8,128)(2,1)S(1)}, bf16[2,3,24,384]{3,2,1,0:T(8,128)(2,1)S(1)}, u32[]{:S(2)}, u32[]{:S(2)}) collective-permute-start(bf16[2,3,24,384]{3,2,1,0:T(8,128)(2,1)S(1)} %get-tuple-element.27), channel_id=1, source_target_pairs={{0,4},{4,0},{1,5},{5,1},{2,6},{6,2},{3,7},{7,3},{8,12},{12,8},{9,1... | collective-permute-start | bytes 331784 | tf_op jit(solution)/shard_map/ppermute | solution.py:264
  41.3 8.3 %collective-permute-start.3 = (bf16[2,15,8,384]{3,2,1,0:T(8,128)(2,1)S(1)}, bf16[2,15,8,384]{3,2,1,0:T(8,128)(2,1)S(1)}, u32[]{:S(2)}, u32[]{:S(2)}) collective-permute-start(bf16[2,15,8,384]{3,2,1,0:T(8,128)(2,1)S(1)} %get-tuple-element.26), channel_id=1, source_target_pairs={{0,1},{1,2},{2,3},{3,0},{4,5},{5,6},{6,7},{7,4},{8,9},{9,10},{10,1... | collective-permute-start | bytes 552968 | tf_op jit(solution)/shard_map/ppermute | solution.py:264
where the time goes:
time: 51 us; the launch traced here: 50.7 us
  Pallas kernels  29.9 us (59%)
  local copies, waits for them, and re-layouts  10.1 us (20%)
  starting transfers between devices  7.42 us (15%)
  waiting for transfers between devices  3.07 us (6%)
    pallas_call x2, Pallas kernels, layer(): pl.pallas_call(functools.partial(layer_kernel, heads, together), grid=(co...  15.1 us
    pallas_call x2, Pallas kernels, call(): pl.pallas_call(functools.partial(bias_kernel, slab, with_rest), out_shape...  11.8 us
    unnamed x22, local copies, waits for them, and re-layouts  7.49 us
    ppermute x2, starting transfers between devices, from_corner(): return lax.ppermute(value, ('lat', 'lon'), pairs)  5.48 us
    ppermute x4, waiting for transfers between devices, from_behind(): return lax.ppermute(value, axis, pairs)  3.06 us
    pallas_call x4, Pallas kernels, small(): pl.pallas_call(kernel, out_shape=shapes, compiler_params=pltpu.CompilerPa...  2.98 us
    ppermute x4, starting transfers between devices, from_behind(): return lax.ppermute(value, axis, pairs)  1.94 us
    reshape x1, local copies, waits for them, and re-layouts, bias_tables(): table = earth_bias.transpose(0, 2, 1).reshape(count, positions)  1.06 us
  transfers between devices with their start and end apart: 6, of which 1 were waited for; matrix products, arithmetic and copies ran while one was open for 1% of the time, Pallas kernels for 24%

commit v1 on v0

v1 whole, which is shorter than its diff:
```python
import functools
import math

import jax
import jax.numpy as jnp
from jax import lax
from jax.experimental import pallas as pl
from jax.experimental.pallas import tpu as pltpu
from jax.sharding import PartitionSpec as P

WZ = 2
WLAT = 6
WLON = 12
HALF_LAT = WLAT // 2
HALF_LON = WLON // 2
EPS_NORM = 1e-05
LOG2E = math.log2(math.e)
LO = 256
LANES = 128
AT_ONCE = 4
GRANT = 48 * 1024 * 1024
NT = (((1,), (1,)), ((), ()))
MESH = pl.DeviceIdType.MESH


def norm_rows(wide):
    average = jnp.mean(wide, axis=-1, keepdims=True)
    centred = wide - average
    spread = jnp.mean(centred * centred, axis=-1, keepdims=True)
    return (centred * lax.rsqrt(spread + EPS_NORM)).astype(jnp.bfloat16)


def build_table(earth, table, slab):
    bands, positions, heads = earth.shape
    for piece in range(table.shape[0] // slab):
        start = piece * LO
        size = min(LO, positions - start)
        parts = [earth[band, start : start + size, :].astype(jnp.float32) for band in range(bands)]
        wide = jnp.concatenate(parts, axis=1)
        wide = jnp.pad(wide, ((0, LO - size), (0, LANES - wide.shape[1])))
        table[piece * slab : (piece + 1) * slab, :] = wide.T[:slab].astype(jnp.bfloat16)


def fill_bias(main_idx, rest_idx, table, bias, slab, step):
    tokens = main_idx.shape[0]
    rest = rest_idx.shape[0]
    pieces = table.shape[0] // slab
    low = lax.broadcasted_iota(jnp.int32, (LO, LANES), 0)

    def lookup(lines):
        spots = [jnp.where(low == (row & (LO - 1)), 1.0, 0.0).astype(jnp.bfloat16) for row in lines]
        found = jnp.dot(
            table[...], jnp.concatenate(spots, axis=1), preferred_element_type=jnp.float32
        )
        picked = []
        for place, row in enumerate(lines):
            high = row // LO
            columns = found[:, place * LANES : (place + 1) * LANES]
            total = columns[(pieces - 1) * slab :]
            for piece in range(pieces - 1):
                total = jnp.where(high == piece, columns[piece * slab : (piece + 1) * slab], total)
            picked.append(total * LOG2E)
        return picked

    @pl.loop(0, tokens // 8)
    def _(block):
        rows = main_idx[pl.ds(pl.multiple_of(block * 8, 8), 8), :]
        for start in range(0, 8, AT_ONCE):
            lines = [rows[start + line : start + line + 1] for line in range(AT_ONCE)]
            for line, values in enumerate(lookup(lines)):
                bias[pl.ds(block * 8 + start + line, slab, stride=step), :] = values

    @pl.loop(0, rest // 8)
    def _(block):
        rows = rest_idx[pl.ds(pl.multiple_of(block * 8, 8), 8), :]
        for start in range(0, 8, AT_ONCE // 2):
            lines = []
            for line in range(start, start + AT_ONCE // 2):
                lines += [rows[line : line + 1, :LANES], rows[line : line + 1, LANES:]]
            for line, values in enumerate(lookup(lines)):
                base = tokens + rest * (line % 2)
                bias[pl.ds(base + block * 8 + start + line // 2, slab, stride=step), :] = values


def attend_window(heads, normed, query, key, row, bias, step, base, w_vt, turned):
    tokens, width = normed.shape
    dim = width // heads
    per = LANES // dim
    rest = tokens - LANES
    scale = dim ** (-0.5) * LOG2E
    value_t = lax.dot_general(w_vt[...], normed, NT, preferred_element_type=jnp.float32)
    value_t = value_t.astype(jnp.bfloat16)
    row = row.astype(jnp.float32)
    diagonal = lax.broadcasted_iota(jnp.int32, (tokens, tokens), 0) == lax.broadcasted_iota(
        jnp.int32, (tokens, tokens), 1
    )
    col = jnp.sum(jnp.where(diagonal, row, 0.0), axis=1, keepdims=True)
    barred = jnp.where(col == row[:, :LANES], 0.0, -jnp.inf)
    owner = lax.broadcasted_iota(jnp.int32, (LANES, LANES), 1) // dim
    zero = jnp.zeros((), jnp.bfloat16)
    for group in range(width // LANES):
        span = slice(group * LANES, (group + 1) * LANES)
        asked = query[:LANES, span]
        stacked = jnp.concatenate([jnp.where(owner == h, asked, zero) for h in range(per)], axis=0)
        raw = lax.dot_general(key[:, span], stacked, NT, preferred_element_type=jnp.float32)
        for h in range(per):
            head = group * per + h
            scores = raw[:, h * LANES : (h + 1) * LANES] * scale
            scores = scores + bias[base + head * step : base + head * step + tokens, :] + barred
            grown = jnp.exp2(scores - jnp.max(scores, axis=0, keepdims=True))
            total = jnp.sum(grown, axis=0, keepdims=True)
            mixed = jnp.dot(
                value_t[head * dim : (head + 1) * dim],
                grown.astype(jnp.bfloat16),
                preferred_element_type=jnp.float32,
            )
            turned[head * dim : (head + 1) * dim, :] = mixed / total
    owner = lax.broadcasted_iota(jnp.int32, (rest, width), 1) // dim
    asked = query[LANES:]
    stacked = jnp.concatenate([jnp.where(owner == h, asked, zero) for h in range(heads)], axis=0)
    scores = lax.dot_general(stacked, key, NT, preferred_element_type=jnp.float32) * scale
    starts = [base + h * step + tokens for h in range(heads)]
    left = jnp.concatenate([bias[start : start + rest, :] for start in starts], axis=0)
    right = jnp.concatenate([bias[start + rest : start + 2 * rest, :] for start in starts], axis=0)
    scores = scores + jnp.concatenate([left, right[:, : tokens - LANES]], axis=1)
    barred = jnp.where(col[LANES:] == row, 0.0, -jnp.inf)
    scores = scores + jnp.concatenate([barred] * heads, axis=0)
    grown = jnp.exp2(scores - jnp.max(scores, axis=1, keepdims=True))
    total = jnp.sum(grown, axis=1, keepdims=True)
    mixed = lax.dot_general(
        grown.astype(jnp.bfloat16), value_t, NT, preferred_element_type=jnp.float32
    )
    mixed = mixed / total
    last = jnp.zeros((rest, width), jnp.float32)
    for h in range(heads):
        last = jnp.where(owner == h, mixed[h * rest : (h + 1) * rest], last)
    return jnp.concatenate([turned[...].T, last], axis=0).astype(jnp.bfloat16)


def window_order(lat_wins, lon_wins):
    last_lat, last_lon = lat_wins - 1, lon_wins - 1
    order = [(t, last_lon) for t in range(lat_wins)]
    order += [(last_lat, b) for b in range(last_lon)]
    return order + [(t, b) for b in range(last_lon) for t in range(last_lat)]


def layer_kernel(
    heads, slab, step, regions, main_idx, rest_idx, fields, earth_far, qkv_far, proj_far, fc1_far,
    fc2_far, out, earth, w_qkv, w_proj, w_fc1, w_fc2, w_vt, table, bias, own, cols, rows, corner,
    wins, turned, cols_out, cols_back, tip_out, tip_back, rows_out, rows_back,
    load_sems, there_sems, here_sems, send_sems, take_sems,
):
    levels, lat_rows, lon_cols, width = own.shape
    lat_wins, lon_wins = lat_rows // WLAT, lon_cols // WLON
    last_lat, last_lon = lat_wins - 1, lon_wins - 1
    spare = corner.shape[2]
    tokens = wins.shape[1]
    dim = width // heads
    order = window_order(lat_wins, lon_wins)
    slot_of = {window: slot for slot, window in enumerate(order)}

    me_lat, me_lon = lax.axis_index("lat"), lax.axis_index("lon")
    lats, lons = lax.axis_size("lat"), lax.axis_size("lon")

    def device(lat, lon):
        return {
            "lat": lax.rem(me_lat + lat + lats, lats), "lon": lax.rem(me_lon + lon + lons, lons)
        }

    barrier = pltpu.get_barrier_semaphore()
    around = [(0, -1), (0, 1), (-1, 0), (1, 0), (-1, -1), (1, 1)]
    for where in around:
        pl.semaphore_signal(barrier, inc=1, device_id=device(*where), device_id_type=MESH)

    far = (earth_far, fields, qkv_far, proj_far, fc1_far, fc2_far)
    near = (earth, own, w_qkv, w_proj, w_fc1, w_fc2)
    loads = [
        pltpu.make_async_copy(source, target, load_sems.at[i])
        for i, (source, target) in enumerate(zip(far, near))
    ]
    for load in loads:
        load.start()

    def remote(source, target, sems, place, where):
        return pltpu.make_async_remote_copy(
            src_ref=source, dst_ref=target, send_sem=sems[0].at[place], recv_sem=sems[1].at[place],
            device_id=device(*where), device_id_type=MESH,
        )

    pl.semaphore_wait(barrier, len(around))
    ahead = []
    for t in range(lat_wins):
        low, high = t * WLAT + HALF_LAT, min((t + 1) * WLAT + HALF_LAT, lat_rows)
        ahead.append(
            remote(
                fields.at[:, low:high, :spare, :], cols.at[:, low:high], (there_sems, here_sems),
                t, (0, -1),
            )
        )
    tops = fields.at[:, :HALF_LAT]
    ahead.append(remote(tops, rows, (there_sems, here_sems), lat_wins, (-1, 0)))
    edge = fields.at[:, :HALF_LAT, :spare, :]
    ahead.append(remote(edge, corner, (there_sems, here_sems), lat_wins + 1, (-1, -1)))
    for copy in ahead[:last_lat]:
        copy.start()
    ahead[-1].start()
    ahead[last_lat].start()
    ahead[lat_wins].start()

    loads[0].wait()
    build_table(earth, table, slab)
    loads[2].wait()
    turn = w_qkv[:, 2 * width :].astype(jnp.float32).T
    w_vt[...] = turn.astype(jnp.bfloat16)

    fill_bias(main_idx, rest_idx, table, bias, slab, step)

    loads[1].wait()

    def gather(t):
        for level in range(levels):
            source = (level + WZ // 2) % levels
            for a in range(t * WLAT, (t + 1) * WLAT):
                away = a - (lat_rows - HALF_LAT)
                kept = own[source, a + HALF_LAT] if away < 0 else rows[source, away]
                halo = cols[source, a + HALF_LAT] if away < 0 else corner[source, away]
                line = [kept.astype(jnp.float32)[HALF_LON:], halo.astype(jnp.float32)[:HALF_LON]]
                line = jnp.concatenate(line, axis=0)
                place = (level * WLAT + a % WLAT) * WLON
                for b in range(lon_wins):
                    wins[slot_of[t, b], place : place + WLON, :] = line[b * WLON : (b + 1) * WLON]

    def send_back(result, t, b, base):
        copies = []
        count = levels * WLAT

        def lines(chosen, start, stop):
            parts = [result[base + k * WLON + start : base + k * WLON + stop] for k in chosen]
            return jnp.concatenate(parts, axis=0).astype(jnp.bfloat16)

        upper = [k for k in range(count) if k % WLAT < HALF_LAT]
        lower = [k for k in range(count) if k % WLAT >= HALF_LAT]
        sems = (send_sems, take_sems)
        if b == last_lon:
            if t < last_lat:
                cols_out[t] = lines(range(count), HALF_LON, WLON)
                copies.append(remote(cols_out.at[t], cols_back.at[t], sems, t, (0, 1)))
            else:
                tip_out[0] = lines(upper, HALF_LON, WLON)
                tip_out[1] = lines(lower, HALF_LON, WLON)
                copies.append(remote(tip_out.at[0], tip_back.at[0], sems, last_lat, (0, 1)))
                copies.append(remote(tip_out.at[1], tip_back.at[1], sems, lat_wins, (1, 1)))
        if t == last_lat:
            rows_out[b] = lines(lower, 0, WLON)
            copies.append(
                remote(rows_out.at[b], rows_back.at[b], sems, lat_wins + 1 + b, (1, 0))
            )
        for copy in copies:
            copy.start()
        return copies

    ready = set()
    returns = []
    for first in range(0, len(order), 2):
        group = order[first : first + 2]
        for t, b in group:
            if t in ready:
                continue
            ready.add(t)
            ahead[t].wait_recv()
            if t == last_lat:
                ahead[lat_wins].wait_recv()
                ahead[lat_wins + 1].wait_recv()
            gather(t)
        taken = wins[first : first + len(group)].reshape(len(group) * tokens, width)
        normed = norm_rows(taken)
        packed = jnp.dot(normed, w_qkv[:, : 2 * width], preferred_element_type=jnp.float32)
        packed = packed.astype(jnp.bfloat16)
        contexts = []
        for place, (t, b) in enumerate(group):
            part = slice(place * tokens, (place + 1) * tokens)
            contexts.append(
                attend_window(
                    heads, normed[part], packed[part, :width], packed[part, width:],
                    regions[t * lon_wins + b], bias, step, t * heads * step, w_vt,
                    turned.at[first + place],
                )
            )
        if first == 0:
            for load in loads[3:]:
                load.wait()
        context = jnp.concatenate(contexts, axis=0)
        projected = jnp.dot(context, w_proj[...], preferred_element_type=jnp.float32)
        projected = projected.astype(jnp.bfloat16).astype(jnp.float32)
        residual = (taken + projected).astype(jnp.bfloat16).astype(jnp.float32)
        normed = norm_rows(residual)
        grown = jnp.dot(normed, w_fc1[...], preferred_element_type=jnp.float32)
        hidden = (0.5 * grown * (1.0 + lax.erf(grown * math.sqrt(0.5)))).astype(jnp.bfloat16)
        summed = residual + jnp.dot(hidden, w_fc2[...], preferred_element_type=jnp.float32)
        wins[first : first + len(group)] = summed.reshape(len(group), tokens, width)
        for place, (t, b) in enumerate(group):
            returns += send_back(summed, t, b, place * tokens)

    for copy in ahead:
        copy.wait_send()
    for copy in returns:
        copy.wait()

    for level in range(levels):
        for r in range(lat_rows):
            if r < HALF_LAT:
                at = level * HALF_LAT + r
                kept = [rows_back[b, at * WLON : (at + 1) * WLON] for b in range(lon_wins)]
                halo = tip_back[1, at * HALF_LON : (at + 1) * HALF_LON]
            else:
                t, a = divmod(r - HALF_LAT, WLAT)
                at = level * WLAT + a
                kept = [wins[slot_of[t, b], at * WLON : (at + 1) * WLON] for b in range(lon_wins)]
                if t < last_lat:
                    halo = cols_back[t, at * HALF_LON : (at + 1) * HALF_LON]
                else:
                    at = level * HALF_LAT + a
                    halo = tip_back[0, at * HALF_LON : (at + 1) * HALF_LON]
            kept[-1] = kept[-1][:HALF_LON]
            line = jnp.concatenate([halo, *kept], axis=0) if r < HALF_LAT else jnp.concatenate(
                [halo.astype(jnp.float32), *kept], axis=0
            )
            out[(level + WZ // 2) % levels, r] = line.astype(jnp.bfloat16)


def local(fields, region_ids, bias_index, earth_bias, w_qkv, w_proj, w_fc1, w_fc2):
    levels, lat_rows, lon_cols, width = fields.shape
    lat_wins, lon_wins = lat_rows // WLAT, lon_cols // WLON
    tokens = levels * WLAT * WLON
    bands, positions, heads = earth_bias.shape
    rest = tokens - LANES
    spare = -(-HALF_LON // 8) * 8
    slab = -(-bands * heads // 8) * 8
    step = tokens + 2 * rest + 8
    pieces = -(-positions // LO)
    regions = region_ids.reshape(levels, lat_wins, WLAT, lon_wins, WLON)
    regions = regions.transpose(1, 3, 0, 2, 4).reshape(lat_wins * lon_wins, 1, tokens)
    main_idx = bias_index[:LANES].T
    rest_idx = jnp.pad(bias_index[LANES:], ((0, 0), (0, 2 * LANES - tokens)))
    count = lat_wins * lon_wins
    lines = levels * WLAT
    bf16, f32 = jnp.bfloat16, jnp.float32
    weights = (w_qkv, w_proj, w_fc1, w_fc2)
    near = pl.BlockSpec(memory_space=pltpu.VMEM)
    far = pl.BlockSpec(memory_space=pltpu.HBM)
    dma = pltpu.SemaphoreType.DMA
    scratch = [
        pltpu.VMEM(earth_bias.shape, bf16),
        *[pltpu.VMEM(weight.shape, bf16) for weight in weights],
        pltpu.VMEM((width, width), bf16),
        pltpu.VMEM((pieces * slab, LO), bf16),
        pltpu.VMEM((slab * step, LANES), f32),
        pltpu.VMEM(fields.shape, bf16),
        pltpu.VMEM((levels, lat_rows, spare, width), bf16),
        pltpu.VMEM((levels, HALF_LAT, lon_cols, width), bf16),
        pltpu.VMEM((levels, HALF_LAT, spare, width), bf16),
        pltpu.VMEM((count, tokens, width), f32),
        pltpu.VMEM((count, width, LANES), f32),
        pltpu.VMEM((max(lat_wins - 1, 1), lines * HALF_LON, width), bf16),
        pltpu.VMEM((max(lat_wins - 1, 1), lines * HALF_LON, width), bf16),
        pltpu.VMEM((2, lines // 2 * HALF_LON, width), bf16),
        pltpu.VMEM((2, lines // 2 * HALF_LON, width), bf16),
        pltpu.VMEM((lon_wins, lines // 2 * WLON, width), bf16),
        pltpu.VMEM((lon_wins, lines // 2 * WLON, width), bf16),
        dma((6,)),
        dma((lat_wins + 2,)),
        dma((lat_wins + 2,)),
        dma((lat_wins + 1 + lon_wins,)),
        dma((lat_wins + 1 + lon_wins,)),
    ]
    return pl.pallas_call(
        functools.partial(layer_kernel, heads, slab, step),
        out_shape=jax.ShapeDtypeStruct(fields.shape, bf16),
        in_specs=[near] * 3 + [far] * 6,
        out_specs=near,
        scratch_shapes=scratch,
        compiler_params=pltpu.CompilerParams(
            vmem_limit_bytes=GRANT, collective_id=0, has_side_effects=True
        ),
        cost_estimate=pl.CostEstimate(
            flops=2 * count * tokens * sum(weight.size for weight in weights),
            bytes_accessed=fields.size * 4 + earth_bias.size * 20,
            transcendentals=count * heads * tokens * tokens,
        ),
        name="layer",
    )(regions, main_idx, rest_idx, fields, earth_bias, *weights)


def solution(mesh):
    return jax.shard_map(
        local,
        mesh=mesh,
        in_specs=(
            P("ens", "lat", "lon", None),
            P(None, "lat", "lon"),
            P(),
            P("lat", None, None),
            P(),
            P(),
            P(),
            P(),
        ),
        out_specs=P("ens", "lat", "lon", None),
        check_vma=False,
    )
```

time: 51 us -> 41 us (0.80)
  starting transfers between devices: 7.42 us -> 0 us
  waiting for transfers between devices: 3.07 us -> 0 us
  Pallas kernels: 29.9 us -> 31.8 us
  local copies, waits for them, and re-layouts: 10.1 us -> 8.75 us
    ppermute x6 -> x0, starting transfers between devices: 7.42 us -> none  [the longest x2 5.48 us: from_corner(): return lax.ppermute(value, ('lat', 'lon'), pairs)]
    ppermute x6 -> x0, waiting for transfers between devices: 3.07 us -> none  [the longest x4 3.06 us: from_behind(): return lax.ppermute(value, axis, pairs)]
    pallas_call x8 -> x1, Pallas kernels: 29.9 us -> 31.8 us  [local(): pl.pallas_call(functools.partial(layer_kernel, heads, slab, step), out_sh...]
    unnamed x22 -> x13, local copies, waits for them, and re-layouts: 7.49 us -> 6.11 us
    reshape x2 -> x0, local copies, waits for them, and re-layouts: 1.26 us -> none  [the longest x1 1.06 us: bias_tables(): table = earth_bias.transpose(0, 2, 1).reshape(count, positions)]
    reshape x2, local copies, waits for them, and re-layouts: 0.11 us -> 0.83 us  [local(): regions = region_ids.reshape(levels, lat_wins, WLAT, lon_wins, WLON)]
    slice x6 -> x2, local copies, waits for them, and re-layouts: 1 us -> 1.71 us  [the longest x1 0.99 us: local(): main_idx = bias_index[:LANES].T]
  transfers between devices with their start and end apart: 6 -> 0, of which waited for: 1 -> 0; matrix products, arithmetic and copies ran while one was open for 1% -> 0% of each run, Pallas kernels for 24% -> 0%
where the time goes in v1:
time: 41 us; the launch traced here: 40.7 us
  Pallas kernels  31.8 us (78%)
  local copies, waits for them, and re-layouts  8.75 us (21%)
    pallas_call x1, Pallas kernels, local(): pl.pallas_call(functools.partial(layer_kernel, heads, slab, step), out_sh...  31.8 us
    unnamed x13, local copies, waits for them, and re-layouts  6.11 us
    slice x1, local copies, waits for them, and re-layouts, local(): main_idx = bias_index[:LANES].T  0.99 us
    reshape x2, local copies, waits for them, and re-layouts, local(): regions = region_ids.reshape(levels, lat_wins, WLAT, lon_wins, WLON)  0.83 us

profile of v1, /device:TPU:0, one launch (start us, length us, event | category | flops | bytes accessed | tf_op | source)
XLA Modules:
  0.0 40.7 jit_solution(5395596282032204686)
XLA Ops:
  0.0 0.7 %slice.7 = s32[16,144]{1,0:T(8,128)S(1)} slice(s32[144,144]{1,0:T(8,128)} %param.10), slice={[128:144], [0:144]} | slice | bytes 18432 | tf_op jit(solution)/shard_map/slice | solution.py:344
  0.7 0.8 %reshape.6 = s32[2,3,6,2,12]{4,3,0,2,1:T(2,128)S(1)} reshape(s32[2,18,24]{2,0,1:T(2,128)} %param.9) | data formatting | bytes 6912 | tf_op jit(solution)/shard_map/reshape | solution.py:341
  1.6 0.1 reshape.8.regions
  1.7 0.0 copy-start.2
  1.7 1.0 %slice.6 = s32[128,144]{1,0:T(8,128)S(1)} slice(s32[144,144]{1,0:T(8,128)} %param.10), slice={[0:128], [0:144]} | slice | bytes 147456 | tf_op jit(solution)/shard_map/slice | solution.py:343
  2.7 0.1 copy.16
  2.8 0.0 copy-start
  2.8 0.0 copy-start.1
  2.8 3.1 %copy.15.earth_far = bf16[3,3312,12]{2,1,0:T(8,128)(2,1)} copy(bf16[3,3312,12]{1,2,0:T(8,128)(2,1)} %param.11) | data formatting | bytes 476928 | tf_op args[3]
  5.9 0.0 copy-done.2
  5.9 0.0 copy-done
  5.9 0.0 copy-done.1
  5.9 0.0 copy-start.3
  5.9 1.1 %copy-done.3 = bf16[2,18,24,384]{3,2,1,0:T(8,128)(2,1)S(1)} copy-done((bf16[2,18,24,384]{3,2,1,0:T(8,128)(2,1)S(1)}, bf16[2,18,24,384]{3,2,1,0:T(8,128)(2,1)}, u32[]{:S(2)}) %copy-start.3) | copy-done | bytes 663576
  7.0 0.0 copy-start.4
  7.0 1.0 %copy-done.4 = bf16[384,384]{1,0:T(8,128)(2,1)S(1)} copy-done((bf16[384,384]{1,0:T(8,128)(2,1)S(1)}, bf16[384,384]{1,0:T(8,128)(2,1)}, u32[]{:S(2)}) %copy-start.4) | copy-done | bytes 294936
  8.0 31.8 %layer.1 = bf16[2,18,24,384]{3,2,1,0:T(8,128)(2,1)S(1)} custom-call(s32[6,1,144]{2,1,0:T(1,128)S(1)} %reshape.8.regions, s32[144,128]{1,0:T(8,128)S(1)} %bitcast.6, s32[16,256]{1,0:T(8,128)S(1)} %pad.4.rest_idx, bf16[2,18,24,384]{3,2,1,0:T(8,128)(2,1)S(1)} %copy-done.3, bf16[3,3312,12]{2,1,0:T(8,128)(2,1)} %copy.15.earth_far, ...), custom_call_target="tpu_custom_call" | custom-call | flops 3057647616 | bytes 3711744 | tf_op jit(solution)/shard_map/layer/pallas_call | solution.py:376
  39.8 0.8 %copy.20 = bf16[2,18,24,384]{3,2,1,0:T(8,128)(2,1)} copy(bf16[2,18,24,384]{3,2,1,0:T(8,128)(2,1)S(1)} %layer.1) | data formatting | bytes 1327104
  (2 shorter events, 0.0 us)
Async XLA Ops:
  1.7 4.2 %copy-start.2 = (bf16[384,1152]{1,0:T(8,128)(2,1)S(1)}, bf16[384,1152]{1,0:T(8,128)(2,1)}, u32[]{:S(2)}) copy-start(bf16[384,1152]{1,0:T(8,128)(2,1)} %qkv_far.1) | copy-start | bytes 2654212
  2.8 3.1 %copy-start = (bf16[384,1536]{1,0:T(8,128)(2,1)S(1)}, bf16[384,1536]{1,0:T(8,128)(2,1)}, u32[]{:S(2)}) copy-start(bf16[384,1536]{1,0:T(8,128)(2,1)} %fc1_far.1) | copy-start | bytes 3538948
  2.8 3.1 %copy-start.1 = (bf16[1536,384]{1,0:T(8,128)(2,1)S(1)}, bf16[1536,384]{1,0:T(8,128)(2,1)}, u32[]{:S(2)}) copy-start(bf16[1536,384]{1,0:T(8,128)(2,1)} %fc2_far.1) | copy-start | bytes 3538948
  5.9 1.1 %copy-start.3 = (bf16[2,18,24,384]{3,2,1,0:T(8,128)(2,1)S(1)}, bf16[2,18,24,384]{3,2,1,0:T(8,128)(2,1)}, u32[]{:S(2)}) copy-start(bf16[2,18,24,384]{3,2,1,0:T(8,128)(2,1)} %fields.1) | copy-start | bytes 1990660
  7.0 1.0 %copy-start.4 = (bf16[384,384]{1,0:T(8,128)(2,1)S(1)}, bf16[384,384]{1,0:T(8,128)(2,1)}, u32[]{:S(2)}) copy-start(bf16[384,384]{1,0:T(8,128)(2,1)} %proj_far.1) | copy-start | bytes 884740

commit v2 on v1

--- a/solution.py
+++ b/solution.py
@@ -18,7 +18,11 @@
 LO = 256
 LANES = 128
 AT_ONCE = 4
-GRANT = 48 * 1024 * 1024
+EARLY = 4
+MOST = (1, 2, 2, 2)
+HEAD = 0
+UNROLL = 7
+GRANT = 64000000
 NT = (((1,), (1,)), ((), ()))
 MESH = pl.DeviceIdType.MESH
 
@@ -31,44 +35,53 @@
 
 
 def build_table(earth, table, slab):
-    bands, positions, heads = earth.shape
+    bands, heads, positions = earth.shape
+    spare = jnp.zeros((slab - bands * heads, LO), jnp.float32)
     for piece in range(table.shape[0] // slab):
         start = piece * LO
         size = min(LO, positions - start)
-        parts = [earth[band, start : start + size, :].astype(jnp.float32) for band in range(bands)]
-        wide = jnp.concatenate(parts, axis=1)
-        wide = jnp.pad(wide, ((0, LO - size), (0, LANES - wide.shape[1])))
-        table[piece * slab : (piece + 1) * slab, :] = wide.T[:slab].astype(jnp.bfloat16)
-
-
-def fill_bias(main_idx, rest_idx, table, bias, slab, step):
+        parts = [earth[band, :, start : start + size].astype(jnp.float32) for band in range(bands)]
+        parts = [jnp.pad(part, ((0, 0), (0, LO - size))) for part in parts]
+        rows = jnp.concatenate([*parts, spare][: bands + (slab > bands * heads)], axis=0)
+        table[piece * slab : (piece + 1) * slab, :] = rows.astype(jnp.bfloat16)
+
+
+def split_index(index, main_idx, rest_idx):
+    tokens = index.shape[0]
+    wide = jnp.pad(index[...], ((0, 0), (0, 2 * LANES - tokens)))
+    main_idx[...] = wide[:LANES].T[:tokens]
+    rest_idx[...] = wide[LANES:]
+
+
+def fill_bias(main_idx, rest_idx, table, bias, slab, step, begin, end, unroll):
     tokens = main_idx.shape[0]
     rest = rest_idx.shape[0]
     pieces = table.shape[0] // slab
-    low = lax.broadcasted_iota(jnp.int32, (LO, LANES), 0)
+    low = lax.broadcasted_iota(jnp.int32, (LO, LANES), 0).astype(jnp.bfloat16)
+    one, zero = jnp.ones((), jnp.bfloat16), jnp.zeros((), jnp.bfloat16)
 
     def lookup(lines):
-        spots = [jnp.where(low == (row & (LO - 1)), 1.0, 0.0).astype(jnp.bfloat16) for row in lines]
-        found = jnp.dot(
-            table[...], jnp.concatenate(spots, axis=1), preferred_element_type=jnp.float32
-        )
-        picked = []
-        for place, row in enumerate(lines):
-            high = row // LO
-            columns = found[:, place * LANES : (place + 1) * LANES]
-            total = columns[(pieces - 1) * slab :]
-            for piece in range(pieces - 1):
-                total = jnp.where(high == piece, columns[piece * slab : (piece + 1) * slab], total)
-            picked.append(total * LOG2E)
-        return picked
-
-    @pl.loop(0, tokens // 8)
+        rows = [(line & (LO - 1)).astype(jnp.bfloat16) for line in lines]
+        spots = jnp.concatenate([jnp.where(low == row, one, zero) for row in rows], axis=1)
+        found = jnp.dot(table[...], spots, preferred_element_type=jnp.float32)
+        high = [line // LO for line in lines]
+        total = [found[:slab, i * LANES : (i + 1) * LANES] for i in range(len(lines))]
+        for piece in range(1, pieces):
+            for i in range(len(lines)):
+                here = found[piece * slab : (piece + 1) * slab, i * LANES : (i + 1) * LANES]
+                total[i] = jnp.where(high[i] == piece, here, total[i])
+        return [values * LOG2E for values in total]
+
+    @pl.loop(begin, end, unroll=math.gcd(end - begin, unroll))
     def _(block):
         rows = main_idx[pl.ds(pl.multiple_of(block * 8, 8), 8), :]
         for start in range(0, 8, AT_ONCE):
             lines = [rows[start + line : start + line + 1] for line in range(AT_ONCE)]
             for line, values in enumerate(lookup(lines)):
                 bias[pl.ds(block * 8 + start + line, slab, stride=step), :] = values
+
+    if end < tokens // 8:
+        return
 
     @pl.loop(0, rest // 8)
     def _(block):
@@ -137,16 +150,26 @@
     return jnp.concatenate([turned[...].T, last], axis=0).astype(jnp.bfloat16)
 
 
-def window_order(lat_wins, lon_wins):
+def window_groups(lat_wins, lon_wins):
     last_lat, last_lon = lat_wins - 1, lon_wins - 1
-    order = [(t, last_lon) for t in range(lat_wins)]
-    order += [(last_lat, b) for b in range(last_lon)]
-    return order + [(t, b) for b in range(last_lon) for t in range(last_lat)]
+    inner = [(t, b) for b in range(last_lon) for t in range(last_lat)]
+    kinds = [
+        inner[:HEAD],
+        [(t, last_lon) for t in range(lat_wins)],
+        [(last_lat, b) for b in range(last_lon)],
+        inner[HEAD:],
+    ]
+    return [
+        kind[first : first + most]
+        for kind, most in zip(kinds, MOST)
+        for first in range(0, len(kind), most)
+    ]
 
 
 def layer_kernel(
-    heads, slab, step, regions, main_idx, rest_idx, fields, earth_far, qkv_far, proj_far, fc1_far,
-    fc2_far, out, earth, w_qkv, w_proj, w_fc1, w_fc2, w_vt, table, bias, own, cols, rows, corner,
+    heads, slab, step, index_far, regions_far, fields, earth_far, qkv_far, proj_far, fc1_far,
+    fc2_far, out, index, regions, earth, w_qkv, w_proj, w_fc1, w_fc2, w_vt, main_idx, rest_idx,
+    table, bias, own, cols, rows, corner,
     wins, turned, cols_out, cols_back, tip_out, tip_back, rows_out, rows_back,
     load_sems, there_sems, here_sems, send_sems, take_sems,
 ):
@@ -156,7 +179,8 @@
     spare = corner.shape[2]
     tokens = wins.shape[1]
     dim = width // heads
-    order = window_order(lat_wins, lon_wins)
+    groups = window_groups(lat_wins, lon_wins)
+    order = sum(groups, [])
     slot_of = {window: slot for slot, window in enumerate(order)}
 
     me_lat, me_lon = lax.axis_index("lat"), lax.axis_index("lon")
@@ -172,8 +196,8 @@
     for where in around:
         pl.semaphore_signal(barrier, inc=1, device_id=device(*where), device_id_type=MESH)
 
-    far = (earth_far, fields, qkv_far, proj_far, fc1_far, fc2_far)
-    near = (earth, own, w_qkv, w_proj, w_fc1, w_fc2)
+    far = (earth_far, index_far, regions_far, fields, qkv_far, proj_far, fc1_far, fc2_far)
+    near = (earth, index, regions, own, w_qkv, w_proj, w_fc1, w_fc2)
     loads = [
         pltpu.make_async_copy(source, target, load_sems.at[i])
         for i, (source, target) in enumerate(zip(far, near))
@@ -187,7 +211,6 @@
             device_id=device(*where), device_id_type=MESH,
         )
 
-    pl.semaphore_wait(barrier, len(around))
     ahead = []
     for t in range(lat_wins):
         low, high = t * WLAT + HALF_LAT, min((t + 1) * WLAT + HALF_LAT, lat_rows)
@@ -201,34 +224,50 @@
     ahead.append(remote(tops, rows, (there_sems, here_sems), lat_wins, (-1, 0)))
     edge = fields.at[:, :HALF_LAT, :spare, :]
     ahead.append(remote(edge, corner, (there_sems, here_sems), lat_wins + 1, (-1, -1)))
+
+    loads[0].wait()
+    build_table(earth, table, slab)
+    loads[1].wait()
+    split_index(index, main_idx, rest_idx)
+    loads[4].wait()
+    turn = w_qkv[:, 2 * width :].astype(jnp.float32).T
+    w_vt[...] = turn.astype(jnp.bfloat16)
+
+    blocks = tokens // 8
+    fill_bias(main_idx, rest_idx, table, bias, slab, step, 0, EARLY, EARLY)
+    pl.semaphore_wait(barrier, len(around))
     for copy in ahead[:last_lat]:
         copy.start()
     ahead[-1].start()
     ahead[last_lat].start()
     ahead[lat_wins].start()
-
-    loads[0].wait()
-    build_table(earth, table, slab)
+    fill_bias(main_idx, rest_idx, table, bias, slab, step, EARLY, blocks, UNROLL)
+
     loads[2].wait()
-    turn = w_qkv[:, 2 * width :].astype(jnp.float32).T
-    w_vt[...] = turn.astype(jnp.bfloat16)
-
-    fill_bias(main_idx, rest_idx, table, bias, slab, step)
-
-    loads[1].wait()
-
-    def gather(t):
+    loads[3].wait()
+
+    def gather(t, b):
+        span = slice(b * WLON, (b + 1) * WLON)
         for level in range(levels):
             source = (level + WZ // 2) % levels
             for a in range(t * WLAT, (t + 1) * WLAT):
                 away = a - (lat_rows - HALF_LAT)
                 kept = own[source, a + HALF_LAT] if away < 0 else rows[source, away]
-                halo = cols[source, a + HALF_LAT] if away < 0 else corner[source, away]
-                line = [kept.astype(jnp.float32)[HALF_LON:], halo.astype(jnp.float32)[:HALF_LON]]
-                line = jnp.concatenate(line, axis=0)
+                line = kept.astype(jnp.float32)[HALF_LON:]
+                if b == last_lon:
+                    halo = cols[source, a + HALF_LAT] if away < 0 else corner[source, away]
+                    line = jnp.concatenate([line, halo.astype(jnp.float32)[:HALF_LON]], axis=0)
                 place = (level * WLAT + a % WLAT) * WLON
-                for b in range(lon_wins):
-                    wins[slot_of[t, b], place : place + WLON, :] = line[b * WLON : (b + 1) * WLON]
+                wins[slot_of[t, b], place : place + WLON, :] = line[span]
+
+    def region_row(t, b):
+        span = slice(b * WLON, (b + 1) * WLON)
+        parts = [
+            regions[t * WLAT + a, level : level + 1, span]
+            for level in range(levels)
+            for a in range(WLAT)
+        ]
+        return jnp.concatenate(parts, axis=1)
 
     def send_back(result, t, b, base):
         copies = []
@@ -261,17 +300,16 @@
 
     ready = set()
     returns = []
-    for first in range(0, len(order), 2):
-        group = order[first : first + 2]
+    for group in groups:
+        first = slot_of[group[0]]
         for t, b in group:
-            if t in ready:
-                continue
-            ready.add(t)
-            ahead[t].wait_recv()
+            needed = {t} if b == last_lon else set()
             if t == last_lat:
-                ahead[lat_wins].wait_recv()
-                ahead[lat_wins + 1].wait_recv()
-            gather(t)
+                needed |= {lat_wins, lat_wins + 1} if b == last_lon else {lat_wins}
+            for which in sorted(needed - ready):
+                ahead[which].wait_recv()
+            ready |= needed
+            gather(t, b)
         taken = wins[first : first + len(group)].reshape(len(group) * tokens, width)
         normed = norm_rows(taken)
         packed = jnp.dot(normed, w_qkv[:, : 2 * width], preferred_element_type=jnp.float32)
@@ -282,12 +320,12 @@
             contexts.append(
                 attend_window(
                     heads, normed[part], packed[part, :width], packed[part, width:],
-                    regions[t * lon_wins + b], bias, step, t * heads * step, w_vt,
+                    region_row(t, b), bias, step, t * heads * step, w_vt,
                     turned.at[first + place],
                 )
             )
-        if first == 0:
-            for load in loads[3:]:
+        if group is groups[0]:
+            for load in loads[5:]:
                 load.wait()
         context = jnp.concatenate(contexts, axis=0)
         projected = jnp.dot(context, w_proj[...], preferred_element_type=jnp.float32)
@@ -338,10 +376,6 @@
     slab = -(-bands * heads // 8) * 8
     step = tokens + 2 * rest + 8
     pieces = -(-positions // LO)
-    regions = region_ids.reshape(levels, lat_wins, WLAT, lon_wins, WLON)
-    regions = regions.transpose(1, 3, 0, 2, 4).reshape(lat_wins * lon_wins, 1, tokens)
-    main_idx = bias_index[:LANES].T
-    rest_idx = jnp.pad(bias_index[LANES:], ((0, 0), (0, 2 * LANES - tokens)))
     count = lat_wins * lon_wins
     lines = levels * WLAT
     bf16, f32 = jnp.bfloat16, jnp.float32
@@ -350,9 +384,13 @@
     far = pl.BlockSpec(memory_space=pltpu.HBM)
     dma = pltpu.SemaphoreType.DMA
     scratch = [
-        pltpu.VMEM(earth_bias.shape, bf16),
+        pltpu.VMEM(bias_index.shape, jnp.int32),
+        pltpu.VMEM((lat_rows, levels, lon_cols), jnp.int32),
+        pltpu.VMEM((bands, heads, positions), bf16),
         *[pltpu.VMEM(weight.shape, bf16) for weight in weights],
         pltpu.VMEM((width, width), bf16),
+        pltpu.VMEM((tokens, LANES), jnp.int32),
+        pltpu.VMEM((rest, 2 * LANES), jnp.int32),
         pltpu.VMEM((pieces * slab, LO), bf16),
         pltpu.VMEM((slab * step, LANES), f32),
         pltpu.VMEM(fields.shape, bf16),
@@ -367,7 +405,7 @@
         pltpu.VMEM((2, lines // 2 * HALF_LON, width), bf16),
         pltpu.VMEM((lon_wins, lines // 2 * WLON, width), bf16),
         pltpu.VMEM((lon_wins, lines // 2 * WLON, width), bf16),
-        dma((6,)),
+        dma((8,)),
         dma((lat_wins + 2,)),
         dma((lat_wins + 2,)),
         dma((lat_wins + 1 + lon_wins,)),
@@ -375,8 +413,8 @@
     ]
     return pl.pallas_call(
         functools.partial(layer_kernel, heads, slab, step),
-        out_shape=jax.ShapeDtypeStruct(fields.shape, bf16),
-        in_specs=[near] * 3 + [far] * 6,
+        out_shape=pltpu.VMEM(fields.shape, bf16),
+        in_specs=[far] * 8,
         out_specs=near,
         scratch_shapes=scratch,
         compiler_params=pltpu.CompilerParams(
@@ -388,7 +426,9 @@
             transcendentals=count * heads * tokens * tokens,
         ),
         name="layer",
-    )(regions, main_idx, rest_idx, fields, earth_bias, *weights)
+    )(
+        bias_index, region_ids.transpose(1, 0, 2), fields, earth_bias.transpose(0, 2, 1), *weights
+    )
 
 
 def solution(mesh):

time: 41 us -> 26.8 us (0.65)
  local copies, waits for them, and re-layouts: 8.75 us -> 0.84 us
  Pallas kernels: 31.8 us -> 25.8 us
    pallas_call x1, Pallas kernels: 31.8 us -> 25.8 us  [local(): pl.pallas_call(functools.partial(layer_kernel, heads, slab, step), out_sh...]
    unnamed x13 -> x1, local copies, waits for them, and re-layouts: 6.11 us -> 0.84 us
    slice x2 -> x0, local copies, waits for them, and re-layouts: 1.71 us -> none  [the longest x1 0.99 us: local(): main_idx = bias_index[:LANES].T]
    reshape x3 -> x0, local copies, waits for them, and re-layouts: 0.92 us -> none  [the longest x2 0.83 us: local(): regions = region_ids.reshape(levels, lat_wins, WLAT, lon_wins, WLON)]
where the time goes in v2:
time: 26.8 us; the launch traced here: 26.6 us
  Pallas kernels  25.8 us (96%)
  local copies, waits for them, and re-layouts  0.84 us (3%)
    pallas_call x1, Pallas kernels, local(): pl.pallas_call(functools.partial(layer_kernel, heads, slab, step), out_sh...  25.8 us
    unnamed x1, local copies, waits for them, and re-layouts  0.84 us

profile of v2, /device:TPU:0, one launch (start us, length us, event | category | flops | bytes accessed | tf_op | source)
XLA Modules:
  0.0 26.6 jit_solution(16567648592073534736)
XLA Ops:
  0.0 25.8 %layer.1 = bf16[2,18,24,384]{3,2,1,0:T(8,128)(2,1)S(1)} custom-call(s32[144,144]{1,0:T(8,128)} %index_far.1, s32[18,2,24]{2,1,0:T(2,128)} %bitcast.3, bf16[2,18,24,384]{3,2,1,0:T(8,128)(2,1)} %fields.1, bf16[3,12,3312]{2,1,0:T(8,128)(2,1)} %bitcast.2, bf16[384,1152]{1,0:T(8,128)(2,1)} %qkv_far.1, bf16[384,384]{1,0:T(8,128)(2,1)} %proj_far.1, ...), custom_call_target="tpu_custom_call" | custom-call | flops 3057647616 | bytes 3711744 | tf_op jit(solution)/shard_map/layer/pallas_call | solution.py:414
  25.8 0.8 %copy.10 = bf16[2,18,24,384]{3,2,1,0:T(8,128)(2,1)} copy(bf16[2,18,24,384]{3,2,1,0:T(8,128)(2,1)S(1)} %layer.1) | data formatting | bytes 1327104

commit v3 on v2

--- a/solution.py
+++ b/solution.py
@@ -18,10 +18,11 @@
 LO = 256
 LANES = 128
 AT_ONCE = 4
-EARLY = 4
-MOST = (1, 2, 2, 2)
+EARLY = 2
+MOST = (2, 2, 2, 2)
 HEAD = 0
-UNROLL = 7
+UNROLL = 8
+CHUNK = 256
 GRANT = 64000000
 NT = (((1,), (1,)), ((), ()))
 MESH = pl.DeviceIdType.MESH
@@ -34,29 +35,55 @@
     return (centred * lax.rsqrt(spread + EPS_NORM)).astype(jnp.bfloat16)
 
 
-def build_table(earth, table, slab):
+def table_rows(count, pieces):
+    whole = count // 8 * 8
+    left = count - whole
+    fold = 8 // left if left else 1
+    tiles = -(-pieces // fold) if left else 0
+    return whole, left, fold, tiles
+
+
+def build_table(earth, table):
     bands, heads, positions = earth.shape
-    spare = jnp.zeros((slab - bands * heads, LO), jnp.float32)
-    for piece in range(table.shape[0] // slab):
+    pieces = -(-positions // LO)
+    whole, left, fold, tiles = table_rows(bands * heads, pieces)
+    ends = []
+    for piece in range(pieces):
         start = piece * LO
         size = min(LO, positions - start)
         parts = [earth[band, :, start : start + size].astype(jnp.float32) for band in range(bands)]
         parts = [jnp.pad(part, ((0, 0), (0, LO - size))) for part in parts]
-        rows = jnp.concatenate([*parts, spare][: bands + (slab > bands * heads)], axis=0)
-        table[piece * slab : (piece + 1) * slab, :] = rows.astype(jnp.bfloat16)
-
-
-def split_index(index, main_idx, rest_idx):
+        rows = jnp.concatenate(parts, axis=0)
+        table[piece * whole : (piece + 1) * whole, :] = rows[:whole].astype(jnp.bfloat16)
+        ends.append(rows[whole:])
+    if left:
+        base = pieces * whole
+        for tile in range(tiles):
+            rows = ends[tile * fold : (tile + 1) * fold]
+            spare = 8 - left * len(rows)
+            if spare:
+                rows = [*rows, jnp.zeros((spare, LO), jnp.float32)]
+            rows = jnp.concatenate(rows, axis=0).astype(jnp.bfloat16)
+            table[base + tile * 8 : base + (tile + 1) * 8, :] = rows
+
+
+def split_index(index, main_idx, left_idx, right_idx):
     tokens = index.shape[0]
+    rest = tokens - LANES
     wide = jnp.pad(index[...], ((0, 0), (0, 2 * LANES - tokens)))
     main_idx[...] = wide[:LANES].T[:tokens]
-    rest_idx[...] = wide[LANES:]
-
-
-def fill_bias(main_idx, rest_idx, table, bias, slab, step, begin, end, unroll):
+    left_idx[...] = wide[LANES:, :LANES]
+    beside = LANES // rest
+    corner = wide[LANES:, LANES:]
+    for line in range(rest // beside):
+        parts = [corner[line * beside + i : line * beside + i + 1, :rest] for i in range(beside)]
+        right_idx[line : line + 1, :] = jnp.concatenate(parts, axis=1)
+
+
+def fill_bias(main_idx, left_idx, right_idx, table, bias, count, pieces, step, begin, end, unroll):
     tokens = main_idx.shape[0]
-    rest = rest_idx.shape[0]
-    pieces = table.shape[0] // slab
+    rest = left_idx.shape[0]
+    whole, left, fold, tiles = table_rows(count, pieces)
     low = lax.broadcasted_iota(jnp.int32, (LO, LANES), 0).astype(jnp.bfloat16)
     one, zero = jnp.ones((), jnp.bfloat16), jnp.zeros((), jnp.bfloat16)
 
@@ -65,12 +92,33 @@
         spots = jnp.concatenate([jnp.where(low == row, one, zero) for row in rows], axis=1)
         found = jnp.dot(table[...], spots, preferred_element_type=jnp.float32)
         high = [line // LO for line in lines]
-        total = [found[:slab, i * LANES : (i + 1) * LANES] for i in range(len(lines))]
+        spans = [slice(i * LANES, (i + 1) * LANES) for i in range(len(lines))]
+        total = [found[:whole, span] for span in spans]
         for piece in range(1, pieces):
-            for i in range(len(lines)):
-                here = found[piece * slab : (piece + 1) * slab, i * LANES : (i + 1) * LANES]
+            for i, span in enumerate(spans):
+                here = found[piece * whole : (piece + 1) * whole, span]
                 total[i] = jnp.where(high[i] == piece, here, total[i])
-        return [values * LOG2E for values in total]
+        if left:
+            base = pieces * whole
+            ends = [found[base : base + 8, span] for span in spans]
+            for tile in range(1, tiles):
+                for i, span in enumerate(spans):
+                    here = found[base + tile * 8 : base + (tile + 1) * 8, span]
+                    ends[i] = jnp.where(high[i] // fold == tile, here, ends[i])
+            for i, end in enumerate(ends):
+                picked = end[:left]
+                for part in range(1, fold):
+                    here = end[part * left : (part + 1) * left]
+                    picked = jnp.where(high[i] % fold == part, here, picked)
+                total[i] = (total[i], picked)
+        else:
+            total = [(values, None) for values in total]
+        return total
+
+    def keep(place, values):
+        bias[pl.ds(place, whole, stride=step), :] = values[0] * LOG2E
+        if left:
+            bias[pl.ds(place + whole * step, left, stride=step), :] = values[1] * LOG2E
 
     @pl.loop(begin, end, unroll=math.gcd(end - begin, unroll))
     def _(block):
@@ -78,21 +126,24 @@
         for start in range(0, 8, AT_ONCE):
             lines = [rows[start + line : start + line + 1] for line in range(AT_ONCE)]
             for line, values in enumerate(lookup(lines)):
-                bias[pl.ds(block * 8 + start + line, slab, stride=step), :] = values
+                keep(block * 8 + start + line, values)
 
     if end < tokens // 8:
         return
 
-    @pl.loop(0, rest // 8)
-    def _(block):
-        rows = rest_idx[pl.ds(pl.multiple_of(block * 8, 8), 8), :]
-        for start in range(0, 8, AT_ONCE // 2):
-            lines = []
-            for line in range(start, start + AT_ONCE // 2):
-                lines += [rows[line : line + 1, :LANES], rows[line : line + 1, LANES:]]
-            for line, values in enumerate(lookup(lines)):
-                base = tokens + rest * (line % 2)
-                bias[pl.ds(base + block * 8 + start + line // 2, slab, stride=step), :] = values
+    for start in range(0, rest, AT_ONCE):
+        lines = [left_idx[line : line + 1, :] for line in range(start, min(start + AT_ONCE, rest))]
+        for line, values in enumerate(lookup(lines)):
+            keep(tokens + start + line, values)
+    beside = LANES // rest
+    lines = [right_idx[line : line + 1, :] for line in range(rest // beside)]
+    for line, values in enumerate(lookup(lines)):
+        for i in range(beside):
+            turned = [
+                part if part is None or i == 0 else pltpu.roll(part, LANES - i * rest, axis=1)
+                for part in values
+            ]
+            keep(tokens + rest + line * beside + i, turned)
 
 
 def attend_window(heads, normed, query, key, row, bias, step, base, w_vt, turned):
@@ -128,6 +179,7 @@
                 preferred_element_type=jnp.float32,
             )
             turned[head * dim : (head + 1) * dim, :] = mixed / total
+        yield
     owner = lax.broadcasted_iota(jnp.int32, (rest, width), 1) // dim
     asked = query[LANES:]
     stacked = jnp.concatenate([jnp.where(owner == h, asked, zero) for h in range(heads)], axis=0)
@@ -147,7 +199,33 @@
     last = jnp.zeros((rest, width), jnp.float32)
     for h in range(heads):
         last = jnp.where(owner == h, mixed[h * rest : (h + 1) * rest], last)
-    return jnp.concatenate([turned[...].T, last], axis=0).astype(jnp.bfloat16)
+    yield jnp.concatenate([turned[...].T, last], axis=0).astype(jnp.bfloat16)
+
+
+def feed_forward(residual, normed, w_fc1, w_fc2):
+    hidden = []
+    for start in range(0, w_fc1.shape[1], CHUNK):
+        grown = jnp.dot(
+            normed, w_fc1[:, start : start + CHUNK], preferred_element_type=jnp.float32
+        )
+        halved = 0.5 * grown * (1.0 + lax.erf(grown * math.sqrt(0.5)))
+        hidden.append(halved.astype(jnp.bfloat16))
+        yield
+    hidden = jnp.concatenate(hidden, axis=1)
+    yield residual + jnp.dot(hidden, w_fc2[...], preferred_element_type=jnp.float32)
+
+
+def weave(*works):
+    steps = [count for work, count in works]
+    done, values = [0] * len(works), [None] * len(works)
+    for _ in range(sum(steps)):
+        which = min(
+            (i for i in range(len(works)) if done[i] < steps[i]),
+            key=lambda i: (done[i] + 0.5) / steps[i],
+        )
+        values[which] = next(works[which][0])
+        done[which] += 1
+    return values
 
 
 def window_groups(lat_wins, lon_wins):
@@ -167,9 +245,9 @@
 
 
 def layer_kernel(
-    heads, slab, step, index_far, regions_far, fields, earth_far, qkv_far, proj_far, fc1_far,
-    fc2_far, out, index, regions, earth, w_qkv, w_proj, w_fc1, w_fc2, w_vt, main_idx, rest_idx,
-    table, bias, own, cols, rows, corner,
+    heads, step, index_far, regions_far, fields, earth_far, qkv_far, proj_far, fc1_far,
+    fc2_far, out, index, regions, earth, w_qkv, w_proj, w_fc1, w_fc2, w_vt, main_idx, left_idx,
+    right_idx, table, bias, own, cols, rows, corner,
     wins, turned, cols_out, cols_back, tip_out, tip_back, rows_out, rows_back,
     load_sems, there_sems, here_sems, send_sems, take_sems,
 ):
@@ -226,22 +304,26 @@
     ahead.append(remote(edge, corner, (there_sems, here_sems), lat_wins + 1, (-1, -1)))
 
     loads[0].wait()
-    build_table(earth, table, slab)
+    build_table(earth, table)
     loads[1].wait()
-    split_index(index, main_idx, rest_idx)
+    split_index(index, main_idx, left_idx, right_idx)
     loads[4].wait()
     turn = w_qkv[:, 2 * width :].astype(jnp.float32).T
     w_vt[...] = turn.astype(jnp.bfloat16)
 
     blocks = tokens // 8
-    fill_bias(main_idx, rest_idx, table, bias, slab, step, 0, EARLY, EARLY)
+    look = functools.partial(
+        fill_bias, main_idx, left_idx, right_idx, table, bias, earth.shape[0] * heads,
+        -(-earth.shape[2] // LO), step,
+    )
+    look(0, EARLY, EARLY)
     pl.semaphore_wait(barrier, len(around))
     for copy in ahead[:last_lat]:
         copy.start()
     ahead[-1].start()
     ahead[last_lat].start()
     ahead[lat_wins].start()
-    fill_bias(main_idx, rest_idx, table, bias, slab, step, EARLY, blocks, UNROLL)
+    look(EARLY, blocks, UNROLL)
 
     loads[2].wait()
     loads[3].wait()
@@ -298,46 +380,62 @@
             copy.start()
         return copies
 
+    for load in loads[5:]:
+        load.wait()
     ready = set()
-    returns = []
-    for group in groups:
-        first = slot_of[group[0]]
+
+    def fetch(group):
+        needed = set()
         for t, b in group:
-            needed = {t} if b == last_lon else set()
+            needed |= {t} if b == last_lon else set()
             if t == last_lat:
                 needed |= {lat_wins, lat_wins + 1} if b == last_lon else {lat_wins}
-            for which in sorted(needed - ready):
-                ahead[which].wait_recv()
-            ready |= needed
+        for which in sorted(needed - ready):
+            ahead[which].wait_recv()
+        ready.update(needed)
+        for t, b in group:
             gather(t, b)
+
+    def attention(group):
+        first = slot_of[group[0]]
         taken = wins[first : first + len(group)].reshape(len(group) * tokens, width)
         normed = norm_rows(taken)
         packed = jnp.dot(normed, w_qkv[:, : 2 * width], preferred_element_type=jnp.float32)
         packed = packed.astype(jnp.bfloat16)
+        yield
         contexts = []
         for place, (t, b) in enumerate(group):
             part = slice(place * tokens, (place + 1) * tokens)
-            contexts.append(
-                attend_window(
-                    heads, normed[part], packed[part, :width], packed[part, width:],
-                    region_row(t, b), bias, step, t * heads * step, w_vt,
-                    turned.at[first + place],
-                )
+            work = attend_window(
+                heads, normed[part], packed[part, :width], packed[part, width:],
+                region_row(t, b), bias, step, t * heads * step, w_vt, turned.at[first + place],
             )
-        if group is groups[0]:
-            for load in loads[5:]:
-                load.wait()
+            for context in work:
+                yield
+            contexts.append(context)
         context = jnp.concatenate(contexts, axis=0)
         projected = jnp.dot(context, w_proj[...], preferred_element_type=jnp.float32)
         projected = projected.astype(jnp.bfloat16).astype(jnp.float32)
         residual = (taken + projected).astype(jnp.bfloat16).astype(jnp.float32)
-        normed = norm_rows(residual)
-        grown = jnp.dot(normed, w_fc1[...], preferred_element_type=jnp.float32)
-        hidden = (0.5 * grown * (1.0 + lax.erf(grown * math.sqrt(0.5)))).astype(jnp.bfloat16)
-        summed = residual + jnp.dot(hidden, w_fc2[...], preferred_element_type=jnp.float32)
-        wins[first : first + len(group)] = summed.reshape(len(group), tokens, width)
-        for place, (t, b) in enumerate(group):
-            returns += send_back(summed, t, b, place * tokens)
+        yield residual, norm_rows(residual)
+
+    returns = []
+    behind = None
+    for group in [*groups, None]:
+        works = []
+        if group is not None:
+            fetch(group)
+            works.append((attention(group), 2 + len(group) * (width // LANES + 1)))
+        if behind is not None:
+            works.append((feed_forward(*passed, w_fc1, w_fc2), w_fc1.shape[1] // CHUNK + 1))
+        values = weave(*works)
+        if behind is not None:
+            summed = values[-1]
+            first = slot_of[behind[0]]
+            wins[first : first + len(behind)] = summed.reshape(len(behind), tokens, width)
+            for place, (t, b) in enumerate(behind):
+                returns += send_back(summed, t, b, place * tokens)
+        behind, passed = group, values[0]
 
     for copy in ahead:
         copy.wait_send()
@@ -373,9 +471,9 @@
     bands, positions, heads = earth_bias.shape
     rest = tokens - LANES
     spare = -(-HALF_LON // 8) * 8
-    slab = -(-bands * heads // 8) * 8
     step = tokens + 2 * rest + 8
     pieces = -(-positions // LO)
+    whole, _, _, tiles = table_rows(bands * heads, pieces)
     count = lat_wins * lon_wins
     lines = levels * WLAT
     bf16, f32 = jnp.bfloat16, jnp.float32
@@ -390,9 +488,10 @@
         *[pltpu.VMEM(weight.shape, bf16) for weight in weights],
         pltpu.VMEM((width, width), bf16),
         pltpu.VMEM((tokens, LANES), jnp.int32),
-        pltpu.VMEM((rest, 2 * LANES), jnp.int32),
-        pltpu.VMEM((pieces * slab, LO), bf16),
-        pltpu.VMEM((slab * step, LANES), f32),
+        pltpu.VMEM((rest, LANES), jnp.int32),
+        pltpu.VMEM((rest * rest // LANES, LANES), jnp.int32),
+        pltpu.VMEM((pieces * whole + 8 * tiles, LO), bf16),
+        pltpu.VMEM((bands * heads * step, LANES), f32),
         pltpu.VMEM(fields.shape, bf16),
         pltpu.VMEM((levels, lat_rows, spare, width), bf16),
         pltpu.VMEM((levels, HALF_LAT, lon_cols, width), bf16),
@@ -412,7 +511,7 @@
         dma((lat_wins + 1 + lon_wins,)),
     ]
     return pl.pallas_call(
-        functools.partial(layer_kernel, heads, slab, step),
+        functools.partial(layer_kernel, heads, step),
         out_shape=pltpu.VMEM(fields.shape, bf16),
         in_specs=[far] * 8,
         out_specs=near,

time: 26.8 us -> 25.2 us (0.940)
  Pallas kernels: 25.8 us -> 24.2 us
    pallas_call x1, Pallas kernels: 25.8 us -> 24.2 us  [local(): pl.pallas_call(functools.partial(layer_kernel, heads, step), out_shape=pl...]
where the time goes in v3:
time: 25.2 us; the launch traced here: 25.1 us
  Pallas kernels  24.2 us (96%)
  local copies, waits for them, and re-layouts  0.84 us (3%)
    pallas_call x1, Pallas kernels, local(): pl.pallas_call(functools.partial(layer_kernel, heads, step), out_shape=pl...  24.2 us
    unnamed x1, local copies, waits for them, and re-layouts  0.84 us

profile of v3, /device:TPU:0, one launch (start us, length us, event | category | flops | bytes accessed | tf_op | source)
XLA Modules:
  0.0 25.1 jit_solution(12199318212111290794)
XLA Ops:
  0.0 24.2 %layer.1 = bf16[2,18,24,384]{3,2,1,0:T(8,128)(2,1)S(1)} custom-call(s32[144,144]{1,0:T(8,128)} %index_far.1, s32[18,2,24]{2,1,0:T(2,128)} %bitcast.3, bf16[2,18,24,384]{3,2,1,0:T(8,128)(2,1)} %fields.1, bf16[3,12,3312]{2,1,0:T(8,128)(2,1)} %bitcast.2, bf16[384,1152]{1,0:T(8,128)(2,1)} %qkv_far.1, bf16[384,384]{1,0:T(8,128)(2,1)} %proj_far.1, ...), custom_call_target="tpu_custom_call" | custom-call | flops 3057647616 | bytes 3711744 | tf_op jit(solution)/shard_map/layer/pallas_call | solution.py:513
  24.2 0.8 %copy.10 = bf16[2,18,24,384]{3,2,1,0:T(8,128)(2,1)} copy(bf16[2,18,24,384]{3,2,1,0:T(8,128)(2,1)S(1)} %layer.1) | data formatting | bytes 1327104

commit v4 on v3

--- a/solution.py
+++ b/solution.py
@@ -19,7 +19,7 @@
 LANES = 128
 AT_ONCE = 4
 EARLY = 2
-MOST = (2, 2, 2, 2)
+MOST = (2, 1, 2, 2)
 HEAD = 0
 UNROLL = 8
 CHUNK = 256
@@ -162,11 +162,20 @@
     barred = jnp.where(col == row[:, :LANES], 0.0, -jnp.inf)
     owner = lax.broadcasted_iota(jnp.int32, (LANES, LANES), 1) // dim
     zero = jnp.zeros((), jnp.bfloat16)
+    raws = []
     for group in range(width // LANES):
         span = slice(group * LANES, (group + 1) * LANES)
         asked = query[:LANES, span]
         stacked = jnp.concatenate([jnp.where(owner == h, asked, zero) for h in range(per)], axis=0)
-        raw = lax.dot_general(key[:, span], stacked, NT, preferred_element_type=jnp.float32)
+        raws.append(
+            lax.dot_general(key[:, span], stacked, NT, preferred_element_type=jnp.float32)
+        )
+    holder = lax.broadcasted_iota(jnp.int32, (rest, width), 1) // dim
+    asked = query[LANES:]
+    stacked = jnp.concatenate([jnp.where(holder == h, asked, zero) for h in range(heads)], axis=0)
+    ends = lax.dot_general(stacked, key, NT, preferred_element_type=jnp.float32)
+    for group in range(width // LANES):
+        raw = raws[group]
         for h in range(per):
             head = group * per + h
             scores = raw[:, h * LANES : (h + 1) * LANES] * scale
@@ -180,10 +189,7 @@
             )
             turned[head * dim : (head + 1) * dim, :] = mixed / total
         yield
-    owner = lax.broadcasted_iota(jnp.int32, (rest, width), 1) // dim
-    asked = query[LANES:]
-    stacked = jnp.concatenate([jnp.where(owner == h, asked, zero) for h in range(heads)], axis=0)
-    scores = lax.dot_general(stacked, key, NT, preferred_element_type=jnp.float32) * scale
+    scores = ends * scale
     starts = [base + h * step + tokens for h in range(heads)]
     left = jnp.concatenate([bias[start : start + rest, :] for start in starts], axis=0)
     right = jnp.concatenate([bias[start + rest : start + 2 * rest, :] for start in starts], axis=0)
@@ -198,7 +204,7 @@
     mixed = mixed / total
     last = jnp.zeros((rest, width), jnp.float32)
     for h in range(heads):
-        last = jnp.where(owner == h, mixed[h * rest : (h + 1) * rest], last)
+        last = jnp.where(holder == h, mixed[h * rest : (h + 1) * rest], last)
     yield jnp.concatenate([turned[...].T, last], axis=0).astype(jnp.bfloat16)
 
 
@@ -403,16 +409,20 @@
         packed = jnp.dot(normed, w_qkv[:, : 2 * width], preferred_element_type=jnp.float32)
         packed = packed.astype(jnp.bfloat16)
         yield
-        contexts = []
+        works = []
         for place, (t, b) in enumerate(group):
             part = slice(place * tokens, (place + 1) * tokens)
-            work = attend_window(
-                heads, normed[part], packed[part, :width], packed[part, width:],
-                region_row(t, b), bias, step, t * heads * step, w_vt, turned.at[first + place],
+            works.append(
+                attend_window(
+                    heads, normed[part], packed[part, :width], packed[part, width:],
+                    region_row(t, b), bias, step, t * heads * step, w_vt, turned.at[first + place],
+                )
             )
-            for context in work:
+        for _ in range(width // LANES + 1):
+            contexts = []
+            for work in works:
+                contexts.append(next(work))
                 yield
-            contexts.append(context)
         context = jnp.concatenate(contexts, axis=0)
         projected = jnp.dot(context, w_proj[...], preferred_element_type=jnp.float32)
         projected = projected.astype(jnp.bfloat16).astype(jnp.float32)

time: 25.2 us -> 22.4 us (0.89)
  Pallas kernels: 24.2 us -> 21.4 us
    pallas_call x1, Pallas kernels: 24.2 us -> 21.4 us  [local(): pl.pallas_call(functools.partial(layer_kernel, heads, step), out_shape=pl...]
where the time goes in v4:
time: 22.4 us; the launch traced here: 22.3 us
  Pallas kernels  21.4 us (96%)
  local copies, waits for them, and re-layouts  0.84 us (4%)
    pallas_call x1, Pallas kernels, local(): pl.pallas_call(functools.partial(layer_kernel, heads, step), out_shape=pl...  21.4 us
    unnamed x1, local copies, waits for them, and re-layouts  0.84 us

profile of v4, /device:TPU:0, one launch (start us, length us, event | category | flops | bytes accessed | tf_op | source)
XLA Modules:
  0.0 22.3 jit_solution(11813832233637420612)
XLA Ops:
  0.0 21.4 %layer.1 = bf16[2,18,24,384]{3,2,1,0:T(8,128)(2,1)S(1)} custom-call(s32[144,144]{1,0:T(8,128)} %index_far.1, s32[18,2,24]{2,1,0:T(2,128)} %bitcast.3, bf16[2,18,24,384]{3,2,1,0:T(8,128)(2,1)} %fields.1, bf16[3,12,3312]{2,1,0:T(8,128)(2,1)} %bitcast.2, bf16[384,1152]{1,0:T(8,128)(2,1)} %qkv_far.1, bf16[384,384]{1,0:T(8,128)(2,1)} %proj_far.1, ...), custom_call_target="tpu_custom_call" | custom-call | flops 3057647616 | bytes 3711744 | tf_op jit(solution)/shard_map/layer/pallas_call | solution.py:523
  21.5 0.8 %copy.10 = bf16[2,18,24,384]{3,2,1,0:T(8,128)(2,1)} copy(bf16[2,18,24,384]{3,2,1,0:T(8,128)(2,1)S(1)} %layer.1) | data formatting | bytes 1327104

commit v5 on v4

--- a/solution.py
+++ b/solution.py
@@ -19,10 +19,11 @@
 LANES = 128
 AT_ONCE = 4
 EARLY = 2
-MOST = (2, 1, 2, 2)
+MOST = (2, 2, 2, 2)
 HEAD = 0
 UNROLL = 8
-CHUNK = 256
+CHUNK = 1536
+SOON = True
 GRANT = 64000000
 NT = (((1,), (1,)), ((), ()))
 MESH = pl.DeviceIdType.MESH
@@ -430,22 +431,38 @@
         yield residual, norm_rows(residual)
 
     returns = []
+
+    def finish(group, summed):
+        first = slot_of[group[0]]
+        wins[first : first + len(group)] = summed.reshape(len(group), tokens, width)
+        copies = []
+        for place, (t, b) in enumerate(group):
+            copies += send_back(summed, t, b, place * tokens)
+        return copies
+
+    def front(group):
+        return attention(group), 2 + len(group) * (width // LANES + 1)
+
+    def back(passed):
+        return feed_forward(*passed, w_fc1, w_fc2), w_fc1.shape[1] // CHUNK + 1
+
     behind = None
-    for group in [*groups, None]:
-        works = []
-        if group is not None:
-            fetch(group)
-            works.append((attention(group), 2 + len(group) * (width // LANES + 1)))
-        if behind is not None:
-            works.append((feed_forward(*passed, w_fc1, w_fc2), w_fc1.shape[1] // CHUNK + 1))
-        values = weave(*works)
-        if behind is not None:
-            summed = values[-1]
-            first = slot_of[behind[0]]
-            wins[first : first + len(behind)] = summed.reshape(len(behind), tokens, width)
-            for place, (t, b) in enumerate(behind):
-                returns += send_back(summed, t, b, place * tokens)
-        behind, passed = group, values[0]
+    for group in groups:
+        fetch(group)
+        if behind is None:
+            (passed,) = weave(front(group))
+        else:
+            ahead_of, summed = weave(front(group), back(passed))
+            returns += finish(behind, summed)
+            passed = ahead_of
+        behind = group
+        if SOON and group[0][1] == last_lon:
+            (summed,) = weave(back(passed))
+            returns += finish(group, summed)
+            behind = None
+    if behind is not None:
+        (summed,) = weave(back(passed))
+        returns += finish(behind, summed)
 
     for copy in ahead:
         copy.wait_send()

time: 22.4 us -> 22.3 us (level)
  no operation moved by 1% of the time
where the time goes in v5:
time: 22.3 us; the launch traced here: 22.1 us
  Pallas kernels  21.3 us (96%)
  local copies, waits for them, and re-layouts  0.84 us (4%)
    pallas_call x1, Pallas kernels, local(): pl.pallas_call(functools.partial(layer_kernel, heads, step), out_shape=pl...  21.3 us
    unnamed x1, local copies, waits for them, and re-layouts  0.84 us

profile of v5, /device:TPU:0, one launch (start us, length us, event | category | flops | bytes accessed | tf_op | source)
XLA Modules:
  0.0 22.1 jit_solution(5003024158895856948)
XLA Ops:
  0.0 21.3 %layer.1 = bf16[2,18,24,384]{3,2,1,0:T(8,128)(2,1)S(1)} custom-call(s32[144,144]{1,0:T(8,128)} %index_far.1, s32[18,2,24]{2,1,0:T(2,128)} %bitcast.3, bf16[2,18,24,384]{3,2,1,0:T(8,128)(2,1)} %fields.1, bf16[3,12,3312]{2,1,0:T(8,128)(2,1)} %bitcast.2, bf16[384,1152]{1,0:T(8,128)(2,1)} %qkv_far.1, bf16[384,384]{1,0:T(8,128)(2,1)} %proj_far.1, ...), custom_call_target="tpu_custom_call" | custom-call | flops 3057647616 | bytes 3711744 | tf_op jit(solution)/shard_map/layer/pallas_call | solution.py:540
  21.3 0.8 %copy.10 = bf16[2,18,24,384]{3,2,1,0:T(8,128)(2,1)} copy(bf16[2,18,24,384]{3,2,1,0:T(8,128)(2,1)S(1)} %layer.1) | data formatting | bytes 1327104
